TPU v7x, 32 devices: a whole 2x2x4 slice. The times are simulated.
32 devices in a mesh: groups: 2 (over x), kv: 16 (over z, y, core).
Axes of the slice: x: 2, y: 2, z: 4, core: 2. Of those that a mesh axis runs over, the one named last changes fastest.
Arguments:
- queries: bfloat16 [80, 18432], P('groups', 'kv'), parts along dimension 0, may hold values from -240 to 240
- latent_cache: bfloat16 [80, 2048, 576], P('groups', 'kv'), parts along dimension 0, may hold values from -6 to 6
- context_lengths: int32 [80], P('groups'), parts along dimension 0, may hold values from 128 to 2048, as said below
- value_up: bfloat16 [16384, 128], P('kv'), may hold values from -0.25 to 0.25
- out_proj: bfloat16 [4096, 7168], P('kv'), may hold values from -0.09375 to 0.09375
- residual: bfloat16 [80, 7168], P('groups', 'kv'), parts along dimension 0, may hold values from -0.75 to 0.75
- norm_gain: bfloat16 [7168], P('kv'), may hold values from 0.5 to 1.5
- expert_ids: int32 [80, 8], P('groups'), parts along dimension 0, may hold values from 0 to 255, all different within a row; in each aligned block of 40 rows (0 to 39, 40 to 79, ...) at most 2 rows name the same one
- gate_weights: float32 [80, 8], P('groups'), parts along dimension 0, may hold values from 0.05 to 0.5
Outputs:
- dispatched: bfloat16 [512, 2, 7168], P(('groups', 'kv')), parts along dimension 0
- slot_scale: float32 [512, 2], P(('groups', 'kv')), parts along dimension 0
- slot_gate: float32 [512, 2], P(('groups', 'kv')), parts along dimension 0
There are 2 independent parts, one for each index of `groups`. A program takes and returns all parts, laid end to end along the dimension named above; an argument that names none is the same for every part. Nothing has to cross between parts.
Inputs may be any that keep to these rules, and one draw needn't show every extreme that they name: `context_lengths`: multiples of 128; some sequence is 2048 long. `expert_ids`: each token names 8 different experts; no expert is named by more than 2 tokens, a bound that some block reaches.
All inputs are finite; a program needn't handle non-finite values. Where the computation divides by a largest or mean magnitude, that divisor is 1e-20 or more.
Results may differ from a plain program's by a relative error of at most 0.0069.
Values may be sent and summed in bfloat16 or wider, within the bound.
No kernel may reach another device: no remote copies, remote signals or barrier semaphores. Data moves between devices by JAX's collectives and lax.ppermute only.
A program may use at most 64 MiB of HBM per device.

v0:
```python
import jax
import jax.numpy as jnp
from jax import lax
from jax.sharding import PartitionSpec as P

H = 32
LAT = 512
ROPE = 64
VD = 128
D = 7168
EXPERTS = 256
TOPK = 8
CAP = 2


score_scale = 192.0 ** (-0.5)
masked_score = -1e30
small_eps = 1e-06


def from_partner(value, axis, bit):
    mask = 2**bit
    pairs = [(source, source ^ mask) for source in range(lax.axis_size(axis))]
    return lax.ppermute(value, axis, pairs)


def slot_targets(expert_ids):
    flat_ids = expert_ids.reshape(-1)
    order_index = jnp.arange(flat_ids.shape[0], dtype=jnp.int32)
    same_before = (flat_ids[:, None] == flat_ids[None, :]) & (
        order_index[None, :] < order_index[:, None]
    )
    rank_within = jnp.sum(same_before.astype(jnp.int32), axis=1)
    return flat_ids * CAP + rank_within


def slot_match(targets, first_slot, slot_count):
    slot_index = first_slot + jnp.arange(slot_count, dtype=jnp.int32)
    return (slot_index[:, None] == targets[None, :]).astype(jnp.float32)


def token_picker(matches, seq_count):
    return jnp.sum(matches.reshape(matches.shape[0], seq_count, TOPK), axis=2)


def per_device(
    queries,
    latent_cache,
    context_lengths,
    value_up,
    out_proj,
    residual,
    norm_gain,
    expert_ids,
    gate_weights,
):
    kv_count = lax.axis_size("kv")
    shard_index = lax.axis_index("kv")
    seq_count = queries.shape[0]
    query_rows = lax.all_gather(queries, "kv", axis=1, tiled=True).reshape(seq_count, H, LAT + ROPE)
    ctx_local = latent_cache.shape[1]
    scores = (
        jnp.einsum("shq,scq->shc", query_rows, latent_cache, preferred_element_type=jnp.float32)
        * score_scale
    )
    position = shard_index * ctx_local + jnp.arange(ctx_local, dtype=jnp.int32)
    valid_mask = (position[None, :] < context_lengths[:, None])[:, None, :]
    scores = jnp.where(valid_mask, scores, masked_score)
    local_max = jnp.max(scores, axis=2)
    weights = jnp.where(valid_mask, jnp.exp(scores - local_max[:, :, None]), 0.0)
    local_total = jnp.sum(weights, axis=2)
    local_out = jnp.einsum(
        "shc,scl->shl",
        weights.astype(jnp.bfloat16),
        latent_cache[:, :, :LAT],
        preferred_element_type=jnp.float32,
    )
    out_rows = out_proj.shape[0]
    col_count = H * LAT // kv_count
    segment = min(col_count, LAT)
    head_count = col_count // segment
    head_start = shard_index * col_count // LAT
    global_max = lax.pmax(local_max, "kv")
    scaling = jnp.exp(local_max - global_max)
    weight_total = lax.psum(local_total * scaling, "kv")
    scaled = (local_out * scaling[:, :, None]).reshape(seq_count, H * LAT)
    merged_sum = lax.psum_scatter(scaled, "kv", scatter_dimension=1, tiled=True).reshape(
        seq_count, head_count, segment
    )
    own_total = lax.dynamic_slice_in_dim(weight_total, head_start, head_count, 1)
    merged = merged_sum / own_total[:, :, None]
    projector = value_up.reshape(head_count, segment, VD).astype(jnp.float32)
    value_part = jnp.einsum("shl,hlv->shv", merged, projector, precision=lax.Precision.HIGHEST)
    holders = kv_count // H if kv_count > H else 1
    for bit in range(holders.bit_length() - 1):
        value_part = value_part + from_partner(value_part, "kv", bit)
    value_rows = value_part.astype(jnp.bfloat16).reshape(seq_count, head_count * VD)
    if holders > 1:
        value_rows = lax.dynamic_slice_in_dim(
            value_rows, shard_index % holders * out_rows, out_rows, 1
        )
    partial_out = jnp.dot(value_rows, out_proj, preferred_element_type=jnp.float32)
    experts_local = EXPERTS // kv_count
    slot_count = experts_local * CAP
    targets = slot_targets(expert_ids)
    own_match = slot_match(targets, shard_index * slot_count, slot_count)
    own_pick = token_picker(own_match, seq_count)
    slot_gate = jnp.dot(own_match, gate_weights.reshape(-1), precision=lax.Precision.HIGHEST)
    attn_rows = lax.psum(partial_out, "kv")
    resid_rows, gain_cols = (
        lax.all_gather(residual, "kv", axis=1, tiled=True),
        lax.all_gather(norm_gain, "kv", axis=0, tiled=True),
    )
    summed = attn_rows + resid_rows.astype(jnp.float32)
    inverse_rms = lax.rsqrt(jnp.mean(summed * summed, axis=1) + small_eps)
    normed = summed * inverse_rms[:, None] * gain_cols.astype(jnp.float32)
    peak_abs = jnp.max(jnp.abs(normed), axis=1) + small_eps
    coded_rows = (normed / peak_abs[:, None]).astype(jnp.bfloat16)
    dispatched = jnp.dot(
        own_pick.astype(jnp.bfloat16), coded_rows, preferred_element_type=jnp.float32
    ).astype(jnp.bfloat16)
    slot_scale = jnp.dot(own_pick, peak_abs, precision=lax.Precision.HIGHEST)
    return (
        dispatched.reshape(experts_local, CAP, D),
        slot_scale.reshape(experts_local, CAP),
        slot_gate.reshape(experts_local, CAP),
    )


def solution(mesh):
    in_specs = (
        P("groups", "kv"),
        P("groups", "kv", None),
        P("groups"),
        P("kv", None),
        P("kv", None),
        P("groups", "kv"),
        P("kv"),
        P("groups", None),
        P("groups", None),
    )
    out_specs = (
        P(("groups", "kv"), None, None),
        P(("groups", "kv"), None),
        P(("groups", "kv"), None),
    )
    return jax.shard_map(
        per_device, mesh=mesh, in_specs=in_specs, out_specs=out_specs, check_vma=False
    )
```

profile of v0, /device:TPU:0, one launch (start us, length us, event | category | flops | bytes accessed | tf_op | source)
XLA Modules:
  0.0 314.2 jit_solution(11004834008479304627)
XLA Ops:
  7.2 0.0 copy-start
  7.2 0.0 all-gather.3.cloned.1.call-start
  7.2 0.7 all-gather.3.cloned.1.call-update
  7.9 0.0 reduce-scatter.2.cloned.1.call-start
  8.0 0.7 broadcast_compare_fusion.1
  8.7 43.6 %all-gather.3.cloned.1.call-done = bf16[40,18432]{1,0:T(8,128)(2,1)} async-done(((bf16[40,1152]{1,0:T(8,128)(2,1)}), bf16[40,18432]{1,0:T(8,128)(2,1)}) %all-gather.3.cloned.1.call-update) | async-done | bytes 1474576 | tf_op jit(solution)/shard_map/all_gather | solution.py:60
  52.3 3.3 %reshape.111 = bf16[40,32,576]{2,1,0:T(8,128)(2,1)S(1)} reshape(bf16[40,18432]{1,0:T(8,128)(2,1)} %all-gather.3.cloned.1.call-done) | data formatting | bytes 2949120 | tf_op jit(solution)/shard_map/reshape | solution.py:60
  55.5 3.9 %fusion.26 = (f32[40,32]{1,0:T(8,128)S(1)}, f32[40,32,128]{2,1,0:T(8,128)S(1)}) fusion(bf16[40,32,576]{2,1,0:T(8,128)(2,1)S(1)} %reshape.111, bf16[40,128,576]{1,2,0:T(8,128)(2,1)} %param.10, pred[40,128]{1,0:T(8,128)(4,1)S(1)} %broadcast_compare_fusion.1), kind=kOutput, calls=%fused_computation.47 | convolution fusion | flops 189233920 | bytes 8038400 | tf_op jit(solution)/shard_map/shq,scq->shc/dot_general | solution.py:63
  59.4 59.5 %pmax.7 = f32[40,32]{1,0:T(8,128)S(1)} all-reduce(f32[40,32]{1,0:T(8,128)S(1)} %get-tuple-element.5), channel_id=1, replica_groups=mesh['groups'=2,'kv'=16] {'kv'}, use_global_device_ids=true, to_apply=%region_3.4 | all-reduce | flops 1280 | bytes 10240 | tf_op jit(solution)/shard_map/pmax | solution.py:83
  118.9 0.4 fusion.7
  119.4 3.9 %fusion.2 = f32[40,32,512]{2,1,0:T(8,128)S(1)} fusion(bf16[40,128,576]{1,2,0:T(8,128)(2,1)} %param.10, f32[40,32]{1,0:T(8,128)S(1)} %get-tuple-element.4, f32[40,32,128]{2,1,0:T(8,128)S(1)} %get-tuple-element.6, f32[40,32]{1,0:T(8,128)S(1)} %get-tuple-element.5, pred[40,128]{1,0:T(8,128)(4,1)S(1)} %broadcast_compare_fusion.1), kind=kOutput, calls=%fused_computation.3 | convolution fusion | flops 168919040 | bytes 8535040 | tf_op jit(solution)/shard_map/shc,scl->shl/dot_general | solution.py:72
  123.3 3.0 copy.51
  126.3 0.0 reduce-scatter.2.cloned.1.call-update
  126.3 0.0 all-reduce.3.cloned.1.call-start
  126.4 0.6 copy-done.3
  127.0 0.1 copy.38
  127.1 0.1 eq.41
  127.2 0.2 convert_reduce_fusion
  127.4 0.1 reduce_sum.39
  127.5 0.1 copy.39
  127.6 19.1 %all-gather = bf16[16,448,40]{1,2,0:T(8,128)(2,1)S(1)} all-gather(bf16[1,448,40]{1,2,0:T(8,128)(2,1)S(1)} %bitcast.43), channel_id=1, replica_groups=mesh['groups'=2,'kv'=16] {'kv'}, dimensions={0}, use_global_device_ids=true | all-gather | bytes 609280 | tf_op jit(solution)/shard_map/all_gather | solution.py:111
  146.7 59.9 %psum.14 = f32[40,32]{1,0:T(8,128)S(1)} all-reduce(f32[40,32]{1,0:T(8,128)S(1)} %get-tuple-element.3), channel_id=1, replica_groups=mesh['groups'=2,'kv'=16] {'kv'}, use_global_device_ids=true, to_apply=%region_6.7 | all-reduce | flops 1280 | bytes 10240 | tf_op jit(solution)/shard_map/psum | solution.py:85
  206.7 0.1 constant_dynamic-slice_fusion
  206.7 1.1 reshape.113
  207.8 0.1 broadcast_divide_fusion
  207.9 0.2 fusion.6
  208.2 3.8 %fusion.17 = f32[40,7168]{1,0:T(8,128)} fusion(bf16[256,7168]{1,0:T(8,128)(2,1)} %param.13, bf16[2,5,8,128]{3,2,1,0:T(8,128)(2,1)S(1)} %fusion.6), kind=kOutput, calls=%fused_computation.28 | convolution fusion | flops 146800640 | bytes 4837376 | tf_op jit(solution)/shard_map/dot_general | solution.py:102
  212.0 0.0 all-reduce.3.cloned.1.call-update
  212.1 0.2 copy.43
  212.3 0.0 copy-start.6
  212.3 0.0 copy-start.5
  212.3 0.5 reshape.125
  212.9 0.1 copy-done.6
  212.9 0.6 dynamic-slice
  214.2 0.3 dynamic-update-slice
  214.4 57.8 %all-reduce = bf16[7168]{0:T(1024)(128)(2,1)S(1)} all-reduce(bf16[7168]{0:T(1024)(128)(2,1)S(1)} %dynamic-update-slice), channel_id=1, replica_groups=mesh['groups'=2,'kv'=16] {'kv'}, use_global_device_ids=true, to_apply=%add | all-reduce | flops 7168 | bytes 28672
  272.3 0.1 copy.44
  272.3 0.1 reshape.128
  272.4 0.1 convert_reduce_fusion.1
  272.6 0.1 broadcast_compare_fusion
  272.7 0.8 fusion.15
  273.5 30.1 %all-reduce.3.cloned.1.call-done = f32[40,7168]{1,0:T(8,128)} async-done(((f32[40,7168]{1,0:T(8,128)}), f32[40,7168]{1,0:T(8,128)}) %all-reduce.3.cloned.1.call-update) | async-done | bytes 1146896 | tf_op jit(solution)/shard_map/psum | solution.py:109
  303.6 1.6 multiply_reduce_fusion
  305.1 0.0 copy-done.1
  305.2 0.4 abs_reduce_fusion
  305.5 0.4 convolution_convert_fusion
  306.0 0.9 reshape.116
  306.9 0.8 fusion.20
  (19 shorter events, 0.1 us)
Async XLA Ops:
  7.2 200.8 %copy-start = (bf16[1024,128]{1,0:T(8,128)(2,1)S(1)}, bf16[1024,128]{1,0:T(8,128)(2,1)}, u32[]{:S(2)}) copy-start(bf16[1024,128]{1,0:T(8,128)(2,1)} %param.12) | copy-start | bytes 786436
  7.2 45.1 %all-gather.3.cloned.1.call-start = ((), (), s32[]{:S(2)}) async-start(), calls=%async_computation.1 | async-start | bytes 1566720 | tf_op jit(solution)/shard_map/all_gather | solution.py:60
  7.9 198.8 %reduce-scatter.2.cloned.1.call-start = ((), (), s32[]{:S(2)}) async-start(), calls=%async_computation.2 | async-start | bytes 2785280 | tf_op jit(solution)/shard_map/reduce_scatter | solution.py:87
  126.3 0.7 copy-start.3
  126.3 1.3 copy-start.2
  126.3 177.2 %all-reduce.3.cloned.1.call-start = ((), (), s32[]{:S(2)}) async-start(), calls=%async_computation.3 | async-start | bytes 2293760 | tf_op jit(solution)/shard_map/psum | solution.py:109
  212.3 0.7 copy-start.6
  212.3 1.9 copy-start.5
  212.3 60.0 %copy-start.4 = (f32[40,8]{0,1:T(8,128)S(1)}, f32[40,8]{0,1:T(8,128)}, u32[]{:S(2)}) copy-start(f32[40,8]{0,1:T(8,128)} %param.17) | copy-start | bytes 3844
  303.6 1.6 copy-start.1
Sparse Core Ops, SparseCore 0:
  10.2 42.0 all-gather.2
  126.5 61.4 reduce-scatter.1
  212.2 91.3 all-reduce.2
where the time goes:
time: 315 us; the launch traced here: 314 us
  blocking collectives  196 us (62%)
  waiting for transfers between devices  74.4 us (24%)
  between operations  14.6 us (5%)
  matrix products  13.9 us (4%)
  local copies, waits for them, and re-layouts  11.1 us (4%)
  other arithmetic  3.74 us (1%)
    psum x1, blocking collectives, per_device(): weight_total = lax.psum(local_total * scaling, 'kv')  59.9 us
    pmax x1, blocking collectives, per_device(): global_max = lax.pmax(local_max, 'kv')  59.5 us
    unnamed x1, blocking collectives  57.8 us
    all_gather x1, waiting for transfers between devices, per_device(): lax.all_gather(queries, 'kv', axis=1, tiled=True)  43.6 us
    psum x1, waiting for transfers between devices, per_device(): attn_rows = lax.psum(partial_out, 'kv')  30.1 us
    all_gather x1, blocking collectives, per_device(): lax.all_gather(residual, 'kv', axis=1, tiled=True)  19.1 us
  transfers between devices with their start and end apart: 3, of which 2 were waited for; matrix products, arithmetic and copies ran while one was open for 1% of the time, Pallas kernels for 0%

commit v1 on v0

--- a/solution.py
+++ b/solution.py
@@ -1,6 +1,8 @@
 import jax
 import jax.numpy as jnp
 from jax import lax
+from jax.experimental import pallas as pl
+from jax.experimental.pallas import tpu as pltpu
 from jax.sharding import PartitionSpec as P
 
 H = 32
@@ -43,7 +45,7 @@
     return jnp.sum(matches.reshape(matches.shape[0], seq_count, TOPK), axis=2)
 
 
-def per_device(
+def split_heads(
     queries,
     latent_cache,
     context_lengths,
@@ -127,6 +129,344 @@
     )
 
 
+LANES = 128
+
+
+def params():
+    return pltpu.CompilerParams(vmem_limit_bytes=56 * 1024 * 1024)
+
+
+def whole(count):
+    return [pl.BlockSpec(memory_space=pltpu.VMEM) for _ in range(count)]
+
+
+def reverse_bits(value, width):
+    result = 0
+    for _ in range(width):
+        result = result * 2 + value % 2
+        value //= 2
+    return result
+
+
+def split_three(values):
+    high = values.astype(jnp.bfloat16).astype(jnp.float32)
+    middle = (values - high).astype(jnp.bfloat16).astype(jnp.float32)
+    return high, middle, values - high - middle
+
+
+def spread_stats(values):
+    high, middle, low = split_three(values)
+    lane = lax.broadcasted_iota(jnp.int32, values.shape, values.ndim - 1)
+    axis = values.ndim - 1
+    parts = jnp.where(lane < 64, pltpu.roll(middle, 32, axis), pltpu.roll(low, 64, axis))
+    return jnp.where(lane < 32, high, parts).astype(jnp.bfloat16)
+
+
+def gather_stats(tile):
+    tile = tile.astype(jnp.float32)
+    axis = tile.ndim - 1
+    return tile + pltpu.roll(tile, LANES - 32, axis) + pltpu.roll(tile, LANES - 64, axis)
+
+
+def attend(place_ref, lengths_ref, own_ref, other_ref, cache_ref, keep_ref, send_ref, q_ref, o_ref):
+    half, seqs, width = own_ref.shape
+    blocks = 2 * half
+    heads = H // blocks
+    ctx_local = cache_ref.shape[1]
+    for block in range(blocks):
+        rows = own_ref[block] if block < half else other_ref[block - half]
+        rows = rows.astype(jnp.float32)
+        for tile in range(width // LANES):
+            q_ref[tile, block * seqs : (block + 1) * seqs, :] = rows[
+                :, tile * LANES : (tile + 1) * LANES
+            ]
+    first = place_ref[0] * ctx_local
+    position = first + lax.broadcasted_iota(jnp.int32, (H, ctx_local), 1)
+    lane = lax.broadcasted_iota(jnp.int32, (blocks, LANES), 1)
+    entry = LAT + ROPE
+
+    def step(seq, carry):
+        mine = pl.ds(seq, blocks, stride=seqs)
+        rows = jnp.concatenate([q_ref[t, mine, :] for t in range(width // LANES)], axis=1)
+        query = jnp.concatenate(
+            [rows[:, h * entry : (h + 1) * entry] for h in range(heads)], axis=0
+        ).astype(jnp.bfloat16)
+        keys = cache_ref[seq]
+        scores = (
+            lax.dot_general(
+                query, keys, (((1,), (1,)), ((), ())), preferred_element_type=jnp.float32
+            )
+            * score_scale
+        )
+        valid = position < lengths_ref[seq]
+        scores = jnp.where(valid, scores, masked_score)
+        top = jnp.max(scores, axis=1, keepdims=True)
+        weights = jnp.where(valid, jnp.exp(scores - top), 0.0)
+        total = jnp.sum(weights, axis=1, keepdims=True)
+        out = lax.dot_general(
+            weights.astype(jnp.bfloat16),
+            keys[:, :LAT],
+            (((1,), (0,)), ((), ())),
+            preferred_element_type=jnp.float32,
+        )
+        stats = jnp.zeros((blocks, LANES), jnp.float32)
+        for h in range(heads):
+            part = slice(h * blocks, (h + 1) * blocks)
+            for t in range(LAT // LANES):
+                o_ref[h * (LAT // LANES) + t, mine, :] = out[part, t * LANES : (t + 1) * LANES]
+            stats = jnp.where(lane == 2 * h, top[part], stats)
+            stats = jnp.where(lane == 2 * h + 1, total[part], stats)
+        o_ref[heads * LAT // LANES, mine, :] = stats
+        return carry
+
+    lax.fori_loop(0, seqs, step, 0, unroll=4)
+    chip = place_ref[0] // 2
+    bits = half.bit_length() - 1
+    for block in range(half):
+        to = chip ^ reverse_bits(block, bits)
+        at = block * seqs
+        past = at + half * seqs
+        last = heads * LAT // LANES
+        for t in range(last):
+            cols = slice(t * LANES, (t + 1) * LANES)
+            keep_ref[to, :, cols] = o_ref[t, at : at + seqs, :]
+            send_ref[to, :, cols] = o_ref[t, past : past + seqs, :].astype(jnp.bfloat16)
+        keep_ref[to, :, heads * LAT :] = o_ref[last, at : at + seqs, :]
+        send_ref[to, :, heads * LAT :] = spread_stats(o_ref[last, past : past + seqs, :])
+
+
+def merge_pair(keep_ref, got_ref, out_ref):
+    half, seqs, width = keep_ref.shape
+    heads = (width - LANES) // LAT
+    lane = lax.broadcasted_iota(jnp.int32, (seqs, LANES), 1)
+
+    def step(block, carry):
+        mine = keep_ref[block, :, heads * LAT :]
+        theirs = gather_stats(got_ref[block, :, heads * LAT :])
+        stats = jnp.zeros((seqs, LANES), jnp.float32)
+        for h in range(heads):
+            top_a, top_b = mine[:, 2 * h : 2 * h + 1], theirs[:, 2 * h : 2 * h + 1]
+            sum_a, sum_b = mine[:, 2 * h + 1 : 2 * h + 2], theirs[:, 2 * h + 1 : 2 * h + 2]
+            top = jnp.maximum(top_a, top_b)
+            scale_a, scale_b = jnp.exp(top_a - top), jnp.exp(top_b - top)
+            total = sum_a * scale_a + sum_b * scale_b
+            cols = slice(h * LAT, (h + 1) * LAT)
+            out_ref[block, :, cols] = (
+                keep_ref[block, :, cols] * scale_a
+                + got_ref[block, :, cols].astype(jnp.float32) * scale_b
+            ).astype(jnp.bfloat16)
+            stats = jnp.where(lane == 2 * h, top, stats)
+            stats = jnp.where(lane == 2 * h + 1, total, stats)
+        out_ref[block, :, heads * LAT :] = spread_stats(stats)
+        return carry
+
+    lax.fori_loop(0, half, step, 0, unroll=2)
+
+
+def project(place_ref, got_ref, up_ref, proj_ref, keep_ref, send_ref):
+    half, seqs, width = got_ref.shape
+    heads = (width - LANES) // LAT
+    stats = [gather_stats(got_ref[c, :, heads * LAT :]) for c in range(half)]
+    values = []
+    for h in range(heads):
+        tops = [s[:, 2 * h : 2 * h + 1] for s in stats]
+        top = tops[0]
+        for t in tops[1:]:
+            top = jnp.maximum(top, t)
+        scales = [jnp.exp(t - top) for t in tops]
+        total = sum(s[:, 2 * h + 1 : 2 * h + 2] * x for s, x in zip(stats, scales))
+        merged = sum(
+            got_ref[c, :, h * LAT : (h + 1) * LAT].astype(jnp.float32) * scales[c]
+            for c in range(half)
+        )
+        merged = merged / total
+        high = merged.astype(jnp.bfloat16)
+        low = (merged - high.astype(jnp.float32)).astype(jnp.bfloat16)
+        up = up_ref[h * LAT : (h + 1) * LAT, :]
+        value = jnp.dot(high, up, preferred_element_type=jnp.float32)
+        value = value + jnp.dot(low, up, preferred_element_type=jnp.float32)
+        values.append(value.astype(jnp.bfloat16))
+    rows = jnp.concatenate(values, axis=1)
+    cols = proj_ref.shape[1] // half
+    part = cols // 2
+    pad = send_ref.shape[2] - part
+    north = place_ref[0] % 2 == 1
+    zeros = jnp.zeros((seqs, pad), jnp.float32)
+    for c in range(half):
+        out = jnp.dot(
+            rows, proj_ref[:, c * cols : (c + 1) * cols], preferred_element_type=jnp.float32
+        )
+        even = jnp.concatenate([out[:, :part], zeros], axis=1)
+        odd = jnp.concatenate([out[:, part:], zeros], axis=1)
+        keep_ref[c] = jnp.where(north, odd, even)
+        send_ref[c] = jnp.where(north, even, odd).astype(jnp.bfloat16)
+
+
+def normalise(got_ref, residual_ref, gain_ref, out_ref):
+    half, seqs, width = got_ref.shape
+    part = residual_ref.shape[1]
+    total = got_ref[0].astype(jnp.float32)
+    for c in range(1, half):
+        total = total + got_ref[c].astype(jnp.float32)
+    summed = total[:, :part] + residual_ref[...].astype(jnp.float32)
+    squares = jnp.sum(summed * summed, axis=1, keepdims=True)
+    gained = summed * gain_ref[...].astype(jnp.float32)
+    peak = jnp.max(jnp.abs(gained), axis=1, keepdims=True)
+    pad = width - part
+    lane = lax.broadcasted_iota(jnp.int32, (seqs, pad), 1)
+    stats = jnp.zeros((seqs, pad), jnp.float32)
+    for at, piece in enumerate(split_three(squares) + split_three(peak)):
+        stats = jnp.where(lane == at, piece, stats)
+    row = jnp.concatenate([gained, stats], axis=1).astype(jnp.bfloat16)
+    for c in range(half):
+        out_ref[c] = row
+
+
+def finish(place_ref, own_ref, other_ref, pick_ref, out_ref, scale_ref):
+    half, seqs, width = own_ref.shape
+    cols = out_ref.shape[1] // half
+    part = cols // 2
+    north = place_ref[0] % 2 == 1
+    squares = jnp.zeros((seqs, 1), jnp.float32)
+    peak = jnp.zeros((seqs, 1), jnp.float32)
+    for ref in (own_ref, other_ref):
+        for c in range(half):
+            stats = ref[c, :, part:].astype(jnp.float32)
+            squares = squares + stats[:, 0:1] + stats[:, 1:2] + stats[:, 2:3]
+            peak = jnp.maximum(peak, stats[:, 3:4] + stats[:, 4:5] + stats[:, 5:6])
+    inverse_rms = lax.rsqrt(squares / (cols * half) + small_eps)
+    peak = peak * inverse_rms + small_eps
+    factor = inverse_rms / peak
+    pick = pick_ref[...]
+    scale_ref[...] = jnp.sum(
+        jnp.where(pick > 0, 1.0, 0.0)
+        * jnp.transpose(jnp.broadcast_to(peak, (seqs, LANES)), (1, 0))[:1, :],
+        axis=1,
+        keepdims=True,
+    )
+    for c in range(half):
+        own, other = own_ref[c, :, :part], other_ref[c, :, :part]
+        pair = jnp.concatenate(
+            [jnp.where(north, other, own), jnp.where(north, own, other)], axis=1
+        )
+        coded = (pair.astype(jnp.float32) * factor).astype(jnp.bfloat16)
+        out_ref[:, c * cols : (c + 1) * cols] = jnp.dot(
+            pick, coded, preferred_element_type=jnp.float32
+        ).astype(jnp.bfloat16)
+
+
+def whole_heads(
+    queries,
+    latent_cache,
+    context_lengths,
+    value_up,
+    out_proj,
+    residual,
+    norm_gain,
+    expert_ids,
+    gate_weights,
+):
+    kv_count = lax.axis_size("kv")
+    shard_index = lax.axis_index("kv")
+    half = kv_count // 2
+    seq_count, width = queries.shape
+    place = shard_index.reshape(1).astype(jnp.int32)
+    chips = [[2 * c + core for c in range(half)] for core in range(2)]
+    smem = pl.BlockSpec(memory_space=pltpu.SMEM)
+
+    def across_chips(value):
+        return lax.all_to_all(value, "kv", 0, 0, axis_index_groups=chips, tiled=True)
+
+    gathered = queries.reshape(1, seq_count, width)
+    for bit in reversed(range(1, kv_count.bit_length() - 1)):
+        gathered = jnp.concatenate([gathered, from_partner(gathered, "kv", bit)], axis=0)
+    other_core = from_partner(gathered, "kv", 0)
+
+    payload = H * LAT // kv_count + LANES
+    block = (half, seq_count, payload)
+    keep, send = pl.pallas_call(
+        attend,
+        name="attend",
+        out_shape=(
+            jax.ShapeDtypeStruct(block, jnp.float32),
+            jax.ShapeDtypeStruct(block, jnp.bfloat16),
+        ),
+        in_specs=[smem, smem] + whole(3),
+        out_specs=tuple(whole(2)),
+        scratch_shapes=[
+            pltpu.VMEM((width // LANES, kv_count * seq_count, LANES), jnp.float32),
+            pltpu.VMEM((payload // LANES, kv_count * seq_count, LANES), jnp.float32),
+        ],
+        compiler_params=params(),
+    )(place, context_lengths, gathered, other_core, latent_cache)
+    got = from_partner(send, "kv", 0)
+    merged = pl.pallas_call(
+        merge_pair,
+        name="merge_pair",
+        out_shape=jax.ShapeDtypeStruct(block, jnp.bfloat16),
+        in_specs=whole(2),
+        out_specs=whole(1)[0],
+        compiler_params=params(),
+    )(keep, got)
+    got = across_chips(merged)
+
+    part = out_proj.shape[1] // kv_count
+    padded = (part + 6 + LANES - 1) // LANES * LANES
+    strip = (half, seq_count, padded)
+    keep, send = pl.pallas_call(
+        project,
+        name="project",
+        out_shape=(
+            jax.ShapeDtypeStruct(strip, jnp.float32),
+            jax.ShapeDtypeStruct(strip, jnp.bfloat16),
+        ),
+        in_specs=[smem] + whole(3),
+        out_specs=tuple(whole(2)),
+        compiler_params=params(),
+    )(place, got, value_up, out_proj)
+    got = from_partner(send, "kv", 0)
+    got = across_chips((keep + got.astype(jnp.float32)).astype(jnp.bfloat16))
+    copies = pl.pallas_call(
+        normalise,
+        name="normalise",
+        out_shape=jax.ShapeDtypeStruct(strip, jnp.bfloat16),
+        in_specs=whole(3),
+        out_specs=whole(1)[0],
+        compiler_params=params(),
+    )(got, residual, norm_gain.reshape(1, part))
+    own = across_chips(copies)
+    other = from_partner(own, "kv", 0)
+
+    experts_local = EXPERTS // kv_count
+    slot_count = experts_local * CAP
+    targets = slot_targets(expert_ids)
+    own_match = slot_match(targets, shard_index * slot_count, slot_count)
+    own_pick = token_picker(own_match, seq_count)
+    slot_gate = jnp.sum(own_match * gate_weights.reshape(1, -1), axis=1)
+    dispatched, slot_scale = pl.pallas_call(
+        finish,
+        name="finish",
+        out_shape=(
+            jax.ShapeDtypeStruct((slot_count, out_proj.shape[1]), jnp.bfloat16),
+            jax.ShapeDtypeStruct((slot_count, 1), jnp.float32),
+        ),
+        in_specs=[smem] + whole(3),
+        out_specs=tuple(whole(2)),
+        compiler_params=params(),
+    )(place, own, other, own_pick.astype(jnp.bfloat16))
+    return (
+        dispatched.reshape(experts_local, CAP, out_proj.shape[1]),
+        slot_scale.reshape(experts_local, CAP),
+        slot_gate.reshape(experts_local, CAP),
+    )
+
+
+def per_device(*args):
+    if lax.axis_size("kv") > H:
+        return split_heads(*args)
+    return whole_heads(*args)
+
+
 def solution(mesh):
     in_specs = (
         P("groups", "kv"),

time: 315 us -> 137 us (0.43)
  blocking collectives: 196 us -> 27.1 us
  waiting for transfers between devices: 74.4 us -> 40.5 us
  Pallas kernels: 0 us -> 30.1 us
  starting transfers between devices: 0.12 us -> 14.2 us
  matrix products: 13.9 us -> 0 us
  between operations: 14.6 us -> 0.72 us
  local copies, waits for them, and re-layouts: 11.1 us -> 16.6 us
    psum x1 -> x0, blocking collectives: 59.9 us -> none  [per_device(): weight_total = lax.psum(local_total * scaling, 'kv')]
    pmax x1 -> x0, blocking collectives: 59.5 us -> none  [per_device(): global_max = lax.pmax(local_max, 'kv')]
    unnamed x1 -> x0, blocking collectives: 57.8 us -> none
    all_gather x1 -> x0, waiting for transfers between devices: 43.6 us -> none  [per_device(): lax.all_gather(queries, 'kv', axis=1, tiled=True)]
    psum x1 -> x0, waiting for transfers between devices: 30.1 us -> none  [per_device(): attn_rows = lax.psum(partial_out, 'kv')]
    pallas_call x0 -> x5, Pallas kernels: none -> 30.1 us  [the longest x1 17.2 us: whole_heads(): pl.pallas_call(attend, name='attend', out_shape=(jax.ShapeDtypeStruct(blo...]
    all_to_all x0 -> x1, blocking collectives: none -> 27.1 us  [across_chips(): lax.all_to_all(value, 'kv', 0, 0, axis_index_groups=chips, tiled=True)]
    ppermute x0 -> x7, waiting for transfers between devices: none -> 21.8 us  [from_partner(): return lax.ppermute(value, axis, pairs)]
  transfers between devices with their start and end apart: 3 -> 9, of which waited for: 2 -> 8; matrix products, arithmetic and copies ran while one was open for 1% -> 9% of each run, Pallas kernels for 0% -> 0%
where the time goes in v1:
time: 137 us; the launch traced here: 136 us
  waiting for transfers between devices  40.5 us (30%)
  Pallas kernels  30.1 us (22%)
  blocking collectives  27.1 us (20%)
  local copies, waits for them, and re-layouts  16.6 us (12%)
  starting transfers between devices  14.2 us (10%)
  other arithmetic  6.7 us (5%)
    all_to_all x1, blocking collectives, across_chips(): lax.all_to_all(value, 'kv', 0, 0, axis_index_groups=chips, tiled=True)  27.1 us
    ppermute x7, waiting for transfers between devices, from_partner(): return lax.ppermute(value, axis, pairs)  21.8 us
    all_to_all x2, waiting for transfers between devices, across_chips(): lax.all_to_all(value, 'kv', 0, 0, axis_index_groups=chips, tiled=True)  18.7 us
    pallas_call x1, Pallas kernels, whole_heads(): pl.pallas_call(attend, name='attend', out_shape=(jax.ShapeDtypeStruct(blo...  17.2 us
    unnamed x23, local copies, waits for them, and re-layouts  13.5 us
    all_to_all x2, starting transfers between devices, across_chips(): lax.all_to_all(value, 'kv', 0, 0, axis_index_groups=chips, tiled=True)  7.21 us
    ppermute x7, starting transfers between devices, from_partner(): return lax.ppermute(value, axis, pairs)  7 us
    pallas_call x1, Pallas kernels, whole_heads(): pl.pallas_call(project, name='project', out_shape=(jax.ShapeDtypeStruct(s...  4.48 us
  transfers between devices with their start and end apart: 9, of which 8 were waited for; matrix products, arithmetic and copies ran while one was open for 9% of the time, Pallas kernels for 0%

profile of v1, /device:TPU:0, one launch (start us, length us, event | category | flops | bytes accessed | tf_op | source)
XLA Modules:
  0.0 135.8 jit_solution(7661445478704302417)
XLA Ops:
  0.6 4.1 %collective-permute-start = (bf16[1,40,1152]{2,1,0:T(8,128)(2,1)}, bf16[1,40,1152]{2,1,0:T(8,128)(2,1)S(1)}, u32[]{:S(2)}, u32[]{:S(2)}) collective-permute-start(bf16[1,40,1152]{2,1,0:T(8,128)(2,1)} %bitcast.2), channel_id=1, source_target_pairs={{0,8},{1,9},{2,10},{3,11},{4,12},{5,13},{6,14},{7,15},{8,0},{9,1},... | collective-permute-start | bytes 276488 | tf_op jit(solution)/shard_map/ppermute | solution.py:26
  4.8 4.8 %collective-permute-done = bf16[1,40,1152]{2,1,0:T(8,128)(2,1)S(1)} collective-permute-done((bf16[1,40,1152]{2,1,0:T(8,128)(2,1)}, bf16[1,40,1152]{2,1,0:T(8,128)(2,1)S(1)}, u32[]{:S(2)}, u32[]{:S(2)}) %collective-permute-start) | collective-permute-done | bytes 92192 | tf_op jit(solution)/shard_map/ppermute | solution.py:26
  9.6 0.9 pad_maximum_fusion.2
  10.5 0.9 collective-permute-start.1
  11.4 4.8 %collective-permute-done.1 = bf16[2,40,1152]{2,1,0:T(8,128)(2,1)S(1)} collective-permute-done((bf16[2,40,1152]{2,1,0:T(8,128)(2,1)S(1)}, bf16[2,40,1152]{2,1,0:T(8,128)(2,1)S(1)}, u32[]{:S(2)}, u32[]{:S(2)}) %collective-permute-start.1) | collective-permute-done | bytes 184352 | tf_op jit(solution)/shard_map/ppermute | solution.py:26
  16.2 0.9 pad_maximum_fusion.1
  17.1 1.6 %collective-permute-start.2 = (bf16[4,40,1152]{2,1,0:T(8,128)(2,1)S(1)}, bf16[4,40,1152]{2,1,0:T(8,128)(2,1)S(1)}, u32[]{:S(2)}, u32[]{:S(2)}) collective-permute-start(bf16[4,40,1152]{2,1,0:T(8,128)(2,1)S(1)} %pad_maximum_fusion.1), channel_id=1, source_target_pairs={{0,2},{1,3},{2,0},{3,1},{4,6},{5,7},{6,4},{7,5},{8,10},{9,11},{10,... | collective-permute-start | bytes 1105928 | tf_op jit(solution)/shard_map/ppermute | solution.py:26
  18.7 7.3 %collective-permute-done.2 = bf16[4,40,1152]{2,1,0:T(8,128)(2,1)S(1)} collective-permute-done((bf16[4,40,1152]{2,1,0:T(8,128)(2,1)S(1)}, bf16[4,40,1152]{2,1,0:T(8,128)(2,1)S(1)}, u32[]{:S(2)}, u32[]{:S(2)}) %collective-permute-start.2) | collective-permute-done | bytes 368672 | tf_op jit(solution)/shard_map/ppermute | solution.py:26
  26.1 1.0 pad_maximum_fusion.own_ref
  27.1 0.1 collective-permute-start.3
  27.1 8.8 %copy.29.cache_ref = bf16[40,128,576]{2,1,0:T(8,128)(2,1)} copy(bf16[40,128,576]{1,2,0:T(8,128)(2,1)} %param.10) | data formatting | bytes 11796480 | tf_op args[1]
  35.9 0.9 copy-done.3
  36.8 17.2 %attend.1 = (f32[8,40,1152]{2,1,0:T(8,128)}, bf16[8,40,1152]{2,1,0:T(8,128)(2,1)}) custom-call(s32[1]{0:T(128)} %bitcast.place_ref, s32[40]{0:T(128)} %lengths_ref.1, bf16[8,40,1152]{2,1,0:T(8,128)(2,1)} %copy-done, bf16[8,40,1152]{2,1,0:T(8,128)(2,1)} %copy-done.3, bf16[40,128,576]{2,1,0:T(8,128)(2,1)} %copy.29.cache_ref), custom_call_target="tpu_custom_call" | custom-call | tf_op jit(solution)/shard_map/attend/pallas_call | solution.py:387
  54.0 0.3 collective-permute-start.4
  54.3 2.1 %collective-permute-done.4.got_ref = bf16[8,40,1152]{2,1,0:T(8,128)(2,1)S(1)} collective-permute-done((bf16[8,40,1152]{2,1,0:T(8,128)(2,1)}, bf16[8,40,1152]{2,1,0:T(8,128)(2,1)S(1)}, u32[]{:S(2)}, u32[]{:S(2)}) %collective-permute-start.4) | collective-permute-done | bytes 737312 | tf_op jit(solution)/shard_map/ppermute | solution.py:26
  56.4 0.9 copy-done.4
  57.3 3.9 %merge_pair.1 = bf16[8,40,1152]{2,1,0:T(8,128)(2,1)} custom-call(f32[8,40,1152]{2,1,0:T(8,128)} %get-tuple-element.9.keep_ref, bf16[8,40,1152]{2,1,0:T(8,128)(2,1)} %copy-done.4), custom_call_target="tpu_custom_call" | custom-call | tf_op jit(solution)/shard_map/merge_pair/pallas_call | solution.py:403
  61.3 27.1 %all_to_all.15.got_ref = bf16[8,40,1152]{2,1,0:T(8,128)(2,1)} all-to-all(bf16[8,40,1152]{2,1,0:T(8,128)(2,1)} %merge_pair.1), channel_id=1, replica_groups={{0,2,4,6,8,10,12,14},{1,3,5,7,9,11,13,15},{16,18,20,22,24,26,28,30},{17..., dimensions={0} | all-to-all | bytes 1474560 | tf_op jit(solution)/shard_map/all_to_all | solution.py:378
  88.4 4.5 %project.1 = (f32[8,40,512]{2,1,0:T(8,128)}, bf16[8,40,512]{2,1,0:T(8,128)(2,1)}) custom-call(s32[1]{0:T(128)} %bitcast.place_ref, bf16[8,40,1152]{2,1,0:T(8,128)(2,1)} %all_to_all.15.got_ref, bf16[1024,128]{1,0:T(8,128)(2,1)} %up_ref.1, bf16[256,7168]{1,0:T(8,128)(2,1)} %proj_ref.1), custom_call_target="tpu_custom_call" | custom-call | tf_op jit(solution)/shard_map/project/pallas_call | solution.py:416
  92.8 0.0 collective-permute-start.5
  92.8 1.8 %collective-permute-done.5 = bf16[8,40,512]{2,1,0:T(8,128)(2,1)S(1)} collective-permute-done((bf16[8,40,512]{2,1,0:T(8,128)(2,1)}, bf16[8,40,512]{2,1,0:T(8,128)(2,1)S(1)}, u32[]{:S(2)}, u32[]{:S(2)}) %collective-permute-start.5) | collective-permute-done | bytes 327712 | tf_op jit(solution)/shard_map/ppermute | solution.py:26
  94.7 1.9 %add_convert_fusion = bf16[8,40,512]{2,1,0:T(8,128)(2,1)} fusion(f32[8,40,512]{2,1,0:T(8,128)} %get-tuple-element.11, bf16[8,40,512]{2,1,0:T(8,128)(2,1)S(1)} %collective-permute-done.5), kind=kLoop, calls=%fused_computation.1 | loop fusion | flops 491520 | bytes 1310720 | tf_op jit(solution)/shard_map/convert_element_type | solution.py:428
  96.6 3.6 %all-to-all-start.1 = ((bf16[8,40,512]{2,1,0:T(8,128)(2,1)}), bf16[8,40,512]{2,1,0:T(8,128)(2,1)S(1)}, u32[]{:S(2)}, u32[]{:S(2)}) async-start(bf16[8,40,512]{2,1,0:T(8,128)(2,1)} %add_convert_fusion), calls=%async_computation.1 | async-start | bytes 655360 | tf_op jit(solution)/shard_map/all_to_all | solution.py:378
  100.2 0.6 reshape.55.gain_ref
  100.8 0.1 copy.30
  100.9 0.1 eq.36
  100.9 9.9 %all-to-all-done.1.got_ref = bf16[8,40,512]{2,1,0:T(8,128)(2,1)S(1)} async-done(((bf16[8,40,512]{2,1,0:T(8,128)(2,1)}), bf16[8,40,512]{2,1,0:T(8,128)(2,1)S(1)}, u32[]{:S(2)}, u32[]{:S(2)}) %all-to-all-start.1) | async-done | bytes 327712 | tf_op jit(solution)/shard_map/all_to_all | solution.py:378
  110.8 0.7 copy-done.2
  111.5 1.9 %normalise.1 = bf16[8,40,512]{2,1,0:T(8,128)(2,1)} custom-call(bf16[8,40,512]{2,1,0:T(8,128)(2,1)} %copy-done.2, bf16[40,448]{1,0:T(8,128)(2,1)} %residual_ref.1, bf16[1,448]{1,0:T(2,128)(2,1)} %reshape.55.gain_ref), custom_call_target="tpu_custom_call" | custom-call | tf_op jit(solution)/shard_map/normalise/pallas_call | solution.py:429
  113.5 3.6 %all-to-all-start.2 = ((bf16[8,40,512]{2,1,0:T(8,128)(2,1)}), bf16[8,40,512]{2,1,0:T(8,128)(2,1)S(1)}, u32[]{:S(2)}, u32[]{:S(2)}) async-start(bf16[8,40,512]{2,1,0:T(8,128)(2,1)} %normalise.1), calls=%async_computation.2 | async-start | bytes 655360 | tf_op jit(solution)/shard_map/all_to_all | solution.py:378
  117.1 0.2 convert_reduce_fusion
  117.3 0.1 reduce_sum.30
  117.4 0.1 copy.31
  117.5 0.1 copy.32
  117.6 0.1 mul.33
  117.7 0.2 select_reduce_fusion
  117.9 0.1 reshape.58
  117.9 0.7 copy.34
  118.6 8.8 %all-to-all-done.2.own_ref = bf16[8,40,512]{2,1,0:T(8,128)(2,1)S(1)} async-done(((bf16[8,40,512]{2,1,0:T(8,128)(2,1)}), bf16[8,40,512]{2,1,0:T(8,128)(2,1)S(1)}, u32[]{:S(2)}, u32[]{:S(2)}) %all-to-all-start.2) | async-done | bytes 327712 | tf_op jit(solution)/shard_map/all_to_all | solution.py:378
  127.4 0.0 collective-permute-start.6
  127.4 0.7 convert_reduce_fusion.1.pick_ref
  128.2 0.9 collective-permute-done.6.other_ref
  129.1 0.7 copy-done.5
  129.8 2.5 %finish.1 = (bf16[32,7168]{1,0:T(8,128)(2,1)}, f32[32,1]{1,0:T(8,128)}) custom-call(s32[1]{0:T(128)} %bitcast.place_ref, bf16[8,40,512]{2,1,0:T(8,128)(2,1)} %copy-done.1, bf16[8,40,512]{2,1,0:T(8,128)(2,1)} %copy-done.5, bf16[32,40]{1,0:T(8,128)(2,1)} %convert_reduce_fusion.1.pick_ref), custom_call_target="tpu_custom_call" | custom-call | tf_op jit(solution)/shard_map/finish/pallas_call | solution.py:446
  132.3 2.0 %reshape.56 = bf16[16,2,7168]{2,1,0:T(2,128)(2,1)} reshape(bf16[32,7168]{1,0:T(8,128)(2,1)} %get-tuple-element.13) | data formatting | bytes 917504 | tf_op jit(solution)/shard_map/reshape | solution.py:458
  134.3 0.8 reduce
  135.1 0.1 reshape.57
  135.2 0.7 copy.33
  (18 shorter events, 0.0 us)
Async XLA Ops:
  0.6 9.0 %collective-permute-start = (bf16[1,40,1152]{2,1,0:T(8,128)(2,1)}, bf16[1,40,1152]{2,1,0:T(8,128)(2,1)S(1)}, u32[]{:S(2)}, u32[]{:S(2)}) collective-permute-start(bf16[1,40,1152]{2,1,0:T(8,128)(2,1)} %bitcast.2), channel_id=1, source_target_pairs={{0,8},{1,9},{2,10},{3,11},{4,12},{5,13},{6,14},{7,15},{8,0},{9,1},... | collective-permute-start | bytes 276488 | tf_op jit(solution)/shard_map/ppermute | solution.py:26
  10.5 5.7 %collective-permute-start.1 = (bf16[2,40,1152]{2,1,0:T(8,128)(2,1)S(1)}, bf16[2,40,1152]{2,1,0:T(8,128)(2,1)S(1)}, u32[]{:S(2)}, u32[]{:S(2)}) collective-permute-start(bf16[2,40,1152]{2,1,0:T(8,128)(2,1)S(1)} %pad_maximum_fusion.2), channel_id=1, source_target_pairs={{0,4},{1,5},{2,6},{3,7},{4,0},{5,1},{6,2},{7,3},{8,12},{9,13},{10,... | collective-permute-start | bytes 552968 | tf_op jit(solution)/shard_map/ppermute | solution.py:26
  17.1 8.9 %collective-permute-start.2 = (bf16[4,40,1152]{2,1,0:T(8,128)(2,1)S(1)}, bf16[4,40,1152]{2,1,0:T(8,128)(2,1)S(1)}, u32[]{:S(2)}, u32[]{:S(2)}) collective-permute-start(bf16[4,40,1152]{2,1,0:T(8,128)(2,1)S(1)} %pad_maximum_fusion.1), channel_id=1, source_target_pairs={{0,2},{1,3},{2,0},{3,1},{4,6},{5,7},{6,4},{7,5},{8,10},{9,11},{10,... | collective-permute-start | bytes 1105928 | tf_op jit(solution)/shard_map/ppermute | solution.py:26
  27.0 8.9 %copy-start = (bf16[8,40,1152]{2,1,0:T(8,128)(2,1)}, bf16[8,40,1152]{2,1,0:T(8,128)(2,1)S(1)}, u32[]{:S(2)}) copy-start(bf16[8,40,1152]{2,1,0:T(8,128)(2,1)S(1)} %pad_maximum_fusion.own_ref) | copy-start | bytes 2211844
  27.1 8.8 %collective-permute-start.3 = (bf16[8,40,1152]{2,1,0:T(8,128)(2,1)S(1)}, bf16[8,40,1152]{2,1,0:T(8,128)(2,1)S(1)}, u32[]{:S(2)}, u32[]{:S(2)}) collective-permute-start(bf16[8,40,1152]{2,1,0:T(8,128)(2,1)S(1)} %pad_maximum_fusion.own_ref), channel_id=1, source_target_pairs={{0,1},{1,0},{2,3},{3,2},{4,5},{5,4},{6,7},{7,6},{8,9},{9,8},{10,11... | collective-permute-start | bytes 2211848 | tf_op jit(solution)/shard_map/ppermute | solution.py:26
  35.9 0.9 copy-start.3
  54.0 46.2 %copy-start.8 = (bf16[448]{0:T(512)(128)(2,1)S(1)}, bf16[448]{0:T(512)(128)(2,1)}, u32[]{:S(2)}) copy-start(bf16[448]{0:T(512)(128)(2,1)} %param.15) | copy-start | bytes 2692
  54.0 46.8 %copy-start.6 = (s32[40,8]{0,1:T(8,128)S(1)}, s32[40,8]{0,1:T(8,128)}, u32[]{:S(2)}) copy-start(s32[40,8]{0,1:T(8,128)} %param.16) | copy-start | bytes 3844
  54.0 2.4 %collective-permute-start.4 = (bf16[8,40,1152]{2,1,0:T(8,128)(2,1)}, bf16[8,40,1152]{2,1,0:T(8,128)(2,1)S(1)}, u32[]{:S(2)}, u32[]{:S(2)}) collective-permute-start(bf16[8,40,1152]{2,1,0:T(8,128)(2,1)} %get-tuple-element.10), channel_id=1, source_target_pairs={{0,1},{1,0},{2,3},{3,2},{4,5},{5,4},{6,7},{7,6},{8,9},{9,8},{10,11... | collective-permute-start | bytes 2211848 | tf_op jit(solution)/shard_map/ppermute | solution.py:26
  56.4 0.9 copy-start.4
  57.3 60.1 %copy-start.7 = (f32[40,8]{0,1:T(8,128)S(1)}, f32[40,8]{0,1:T(8,128)}, u32[]{:S(2)}) copy-start(f32[40,8]{0,1:T(8,128)} %param.17) | copy-start | bytes 3844
  92.8 1.8 %collective-permute-start.5 = (bf16[8,40,512]{2,1,0:T(8,128)(2,1)}, bf16[8,40,512]{2,1,0:T(8,128)(2,1)S(1)}, u32[]{:S(2)}, u32[]{:S(2)}) collective-permute-start(bf16[8,40,512]{2,1,0:T(8,128)(2,1)} %get-tuple-element.12), channel_id=1, source_target_pairs={{0,1},{1,0},{2,3},{3,2},{4,5},{5,4},{6,7},{7,6},{8,9},{9,8},{10,11... | collective-permute-start | bytes 983048 | tf_op jit(solution)/shard_map/ppermute | solution.py:26
  96.6 14.2 %all-to-all-start.1 = ((bf16[8,40,512]{2,1,0:T(8,128)(2,1)}), bf16[8,40,512]{2,1,0:T(8,128)(2,1)S(1)}, u32[]{:S(2)}, u32[]{:S(2)}) async-start(bf16[8,40,512]{2,1,0:T(8,128)(2,1)} %add_convert_fusion), calls=%async_computation.1 | async-start | bytes 655360 | tf_op jit(solution)/shard_map/all_to_all | solution.py:378
  110.8 0.7 copy-start.2
  113.5 14.0 %all-to-all-start.2 = ((bf16[8,40,512]{2,1,0:T(8,128)(2,1)}), bf16[8,40,512]{2,1,0:T(8,128)(2,1)S(1)}, u32[]{:S(2)}, u32[]{:S(2)}) async-start(bf16[8,40,512]{2,1,0:T(8,128)(2,1)} %normalise.1), calls=%async_computation.2 | async-start | bytes 655360 | tf_op jit(solution)/shard_map/all_to_all | solution.py:378
  127.4 1.6 %copy-start.1 = (bf16[8,40,512]{2,1,0:T(8,128)(2,1)}, bf16[8,40,512]{2,1,0:T(8,128)(2,1)S(1)}, u32[]{:S(2)}) copy-start(bf16[8,40,512]{2,1,0:T(8,128)(2,1)S(1)} %all-to-all-done.2.own_ref) | copy-start | bytes 983044
  127.4 1.6 %collective-permute-start.6 = (bf16[8,40,512]{2,1,0:T(8,128)(2,1)S(1)}, bf16[8,40,512]{2,1,0:T(8,128)(2,1)S(1)}, u32[]{:S(2)}, u32[]{:S(2)}) collective-permute-start(bf16[8,40,512]{2,1,0:T(8,128)(2,1)S(1)} %all-to-all-done.2.own_ref), channel_id=1, source_target_pairs={{0,1},{1,0},{2,3},{3,2},{4,5},{5,4},{6,7},{7,6},{8,9},{9,8},{10,11... | collective-permute-start | bytes 983048 | tf_op jit(solution)/shard_map/ppermute | solution.py:26
  129.1 0.7 copy-start.5

commit v2 on v1

--- a/solution.py
+++ b/solution.py
@@ -132,20 +132,48 @@
 LANES = 128
 
 
-def params():
-    return pltpu.CompilerParams(vmem_limit_bytes=56 * 1024 * 1024)
+def params(mebibytes=8):
+    return pltpu.CompilerParams(vmem_limit_bytes=mebibytes * 1024 * 1024)
 
 
 def whole(count):
     return [pl.BlockSpec(memory_space=pltpu.VMEM) for _ in range(count)]
 
 
-def reverse_bits(value, width):
-    result = 0
-    for _ in range(width):
-        result = result * 2 + value % 2
-        value //= 2
-    return result
+def exchange_orders(width):
+    falling = list(range(width - 1, 0, -1))
+    return [falling[-1:] + falling[:-1], falling]
+
+
+def from_crossing(value, steps):
+    pairs = [(source, source ^ 2 ** steps[source % 2]) for source in range(lax.axis_size("kv"))]
+    return lax.ppermute(value, "kv", pairs)
+
+
+def distance(position, order):
+    mask = 0
+    for step, bit in enumerate(order):
+        mask ^= (position >> step) % 2 * 2 ** (bit - 1)
+    return mask
+
+
+def join(*refs):
+    out_ref, at = refs[-1], 0
+    for ref in refs[:-1]:
+        out_ref[at : at + ref.shape[0]] = ref[...]
+        at += ref.shape[0]
+
+
+def joined(parts):
+    count = sum(part.shape[0] for part in parts)
+    return pl.pallas_call(
+        join,
+        name="join",
+        out_shape=jax.ShapeDtypeStruct((count,) + parts[0].shape[1:], parts[0].dtype),
+        in_specs=whole(len(parts)),
+        out_specs=whole(1)[0],
+        compiler_params=params(),
+    )(*parts)
 
 
 def split_three(values):
@@ -168,71 +196,87 @@
     return tile + pltpu.roll(tile, LANES - 32, axis) + pltpu.roll(tile, LANES - 64, axis)
 
 
-def attend(place_ref, lengths_ref, own_ref, other_ref, cache_ref, keep_ref, send_ref, q_ref, o_ref):
-    half, seqs, width = own_ref.shape
+SEQS_AT_ONCE = 4
+
+
+def attend(place_ref, lengths_ref, cache_ref, *refs):
+    pieces, (keep_ref, send_ref, q_ref, o_ref) = refs[:-4], refs[-4:]
+    half, seqs, payload = keep_ref.shape
     blocks = 2 * half
     heads = H // blocks
-    ctx_local = cache_ref.shape[1]
-    for block in range(blocks):
-        rows = own_ref[block] if block < half else other_ref[block - half]
-        rows = rows.astype(jnp.float32)
-        for tile in range(width // LANES):
-            q_ref[tile, block * seqs : (block + 1) * seqs, :] = rows[
-                :, tile * LANES : (tile + 1) * LANES
-            ]
+    entry, ctx_local = cache_ref.shape[1:]
+    tiles = q_ref.shape[1]
+    at = 0
+    for ref in pieces:
+        for block in range(ref.shape[0]):
+            rows = ref[block].astype(jnp.float32)
+            for h in range(heads):
+                for t in range(tiles):
+                    cols = slice(h * entry + t * LANES, h * entry + min((t + 1) * LANES, entry))
+                    q_ref[h, t, at : at + seqs, : cols.stop - cols.start] = rows[:, cols]
+            at += seqs
     first = place_ref[0] * ctx_local
     position = first + lax.broadcasted_iota(jnp.int32, (H, ctx_local), 1)
     lane = lax.broadcasted_iota(jnp.int32, (blocks, LANES), 1)
-    entry = LAT + ROPE
-
-    def step(seq, carry):
-        mine = pl.ds(seq, blocks, stride=seqs)
-        rows = jnp.concatenate([q_ref[t, mine, :] for t in range(width // LANES)], axis=1)
-        query = jnp.concatenate(
-            [rows[:, h * entry : (h + 1) * entry] for h in range(heads)], axis=0
-        ).astype(jnp.bfloat16)
-        keys = cache_ref[seq]
-        scores = (
-            lax.dot_general(
-                query, keys, (((1,), (1,)), ((), ())), preferred_element_type=jnp.float32
+
+    def batch(number, carry):
+        all_seqs = [number * SEQS_AT_ONCE + i for i in range(SEQS_AT_ONCE)]
+        scores, tops, totals, weights, outs = [], [], [], [], []
+        for seq in all_seqs:
+            mine = pl.ds(seq, blocks, stride=seqs)
+            query = jnp.concatenate(
+                [
+                    jnp.concatenate([q_ref[h, t, mine, :] for t in range(tiles)], axis=1)
+                    for h in range(heads)
+                ],
+                axis=0,
+            )[:, :entry].astype(jnp.bfloat16)
+            scores.append(jnp.dot(query, cache_ref[seq], preferred_element_type=jnp.float32))
+        for seq, score in zip(all_seqs, scores):
+            valid = position < lengths_ref[seq]
+            score = jnp.where(valid, score * score_scale, masked_score)
+            top = jnp.max(score, axis=1, keepdims=True)
+            weight = jnp.where(valid, jnp.exp(score - top), 0.0)
+            tops.append(top)
+            totals.append(jnp.sum(weight, axis=1, keepdims=True))
+            weights.append(weight.astype(jnp.bfloat16))
+        for seq, weight in zip(all_seqs, weights):
+            outs.append(
+                lax.dot_general(
+                    weight,
+                    cache_ref[seq, :LAT, :],
+                    (((1,), (1,)), ((), ())),
+                    preferred_element_type=jnp.float32,
+                )
             )
-            * score_scale
-        )
-        valid = position < lengths_ref[seq]
-        scores = jnp.where(valid, scores, masked_score)
-        top = jnp.max(scores, axis=1, keepdims=True)
-        weights = jnp.where(valid, jnp.exp(scores - top), 0.0)
-        total = jnp.sum(weights, axis=1, keepdims=True)
-        out = lax.dot_general(
-            weights.astype(jnp.bfloat16),
-            keys[:, :LAT],
-            (((1,), (0,)), ((), ())),
-            preferred_element_type=jnp.float32,
-        )
-        stats = jnp.zeros((blocks, LANES), jnp.float32)
-        for h in range(heads):
-            part = slice(h * blocks, (h + 1) * blocks)
-            for t in range(LAT // LANES):
-                o_ref[h * (LAT // LANES) + t, mine, :] = out[part, t * LANES : (t + 1) * LANES]
-            stats = jnp.where(lane == 2 * h, top[part], stats)
-            stats = jnp.where(lane == 2 * h + 1, total[part], stats)
-        o_ref[heads * LAT // LANES, mine, :] = stats
+        for seq, top, total, out in zip(all_seqs, tops, totals, outs):
+            mine = pl.ds(seq, blocks, stride=seqs)
+            stats = jnp.zeros((blocks, LANES), jnp.float32)
+            for h in range(heads):
+                part = slice(h * blocks, (h + 1) * blocks)
+                for t in range(LAT // LANES):
+                    o_ref[h * (LAT // LANES) + t, mine, :] = out[part, t * LANES : (t + 1) * LANES]
+                stats = jnp.where(lane == 2 * h, top[part], stats)
+                stats = jnp.where(lane == 2 * h + 1, total[part], stats)
+            o_ref[heads * LAT // LANES, mine, :] = stats
         return carry
 
-    lax.fori_loop(0, seqs, step, 0, unroll=4)
-    chip = place_ref[0] // 2
-    bits = half.bit_length() - 1
+    lax.fori_loop(0, seqs // SEQS_AT_ONCE, batch, 0)
+    chip, north = place_ref[0] // 2, place_ref[0] % 2 == 1
+    orders = exchange_orders(blocks.bit_length() - 1)
+    last = heads * LAT // LANES
     for block in range(half):
-        to = chip ^ reverse_bits(block, bits)
+        even, odd = (distance(block, order) for order in orders)
+        to = chip ^ jnp.where(north, odd, even)
         at = block * seqs
-        past = at + half * seqs
-        last = heads * LAT // LANES
+        for t in range(last + 1):
+            keep_ref[to, :, t * LANES : (t + 1) * LANES] = o_ref[t, at : at + seqs, :]
+        to = chip ^ jnp.where(north, even, odd)
+        at = (half + block) * seqs
         for t in range(last):
             cols = slice(t * LANES, (t + 1) * LANES)
-            keep_ref[to, :, cols] = o_ref[t, at : at + seqs, :]
-            send_ref[to, :, cols] = o_ref[t, past : past + seqs, :].astype(jnp.bfloat16)
-        keep_ref[to, :, heads * LAT :] = o_ref[last, at : at + seqs, :]
-        send_ref[to, :, heads * LAT :] = spread_stats(o_ref[last, past : past + seqs, :])
+            send_ref[to, :, cols] = o_ref[t, at : at + seqs, :].astype(jnp.bfloat16)
+        send_ref[to, :, heads * LAT :] = spread_stats(o_ref[last, at : at + seqs, :])
 
 
 def merge_pair(keep_ref, got_ref, out_ref):
@@ -322,9 +366,33 @@
         out_ref[c] = row
 
 
+def route(place_ref, ids_ref, gates_ref, pick_ref, gate_ref):
+    count, seqs = ids_ref.shape
+    experts = gate_ref.shape[1]
+    expert = place_ref[0] * experts + lax.broadcasted_iota(jnp.int32, (experts, seqs), 0)
+    named = jnp.zeros((experts, seqs), jnp.float32)
+    gates = jnp.zeros((experts, seqs), jnp.float32)
+    for k in range(count):
+        same = ids_ref[k : k + 1, :] == expert
+        named = jnp.where(same, 1.0, named)
+        gates = jnp.where(same, gates_ref[k : k + 1, :], gates)
+    earlier = lax.broadcasted_iota(jnp.int32, (seqs, seqs), 0)
+    later = lax.broadcasted_iota(jnp.int32, (seqs, seqs), 1)
+    before = jnp.where(earlier < later, 1.0, 0.0).astype(jnp.bfloat16)
+    slot = jnp.dot(named.astype(jnp.bfloat16), before, preferred_element_type=jnp.float32)
+    picks, rows = [], []
+    for c in range(CAP):
+        pick = jnp.where(slot == c, named, 0.0)
+        picks.append(pick)
+        chosen = jnp.sum(pick * gates, axis=1, keepdims=True)
+        rows.append(jnp.transpose(jnp.broadcast_to(chosen, (experts, LANES)), (1, 0))[:1])
+    gate_ref[...] = jnp.concatenate(rows, axis=0)
+    pick_ref[...] = jnp.concatenate(picks, axis=0)
+
+
 def finish(place_ref, own_ref, other_ref, pick_ref, out_ref, scale_ref):
     half, seqs, width = own_ref.shape
-    cols = out_ref.shape[1] // half
+    cols = out_ref.shape[2] // half
     part = cols // 2
     north = place_ref[0] % 2 == 1
     squares = jnp.zeros((seqs, 1), jnp.float32)
@@ -337,22 +405,23 @@
     inverse_rms = lax.rsqrt(squares / (cols * half) + small_eps)
     peak = peak * inverse_rms + small_eps
     factor = inverse_rms / peak
-    pick = pick_ref[...]
-    scale_ref[...] = jnp.sum(
-        jnp.where(pick > 0, 1.0, 0.0)
-        * jnp.transpose(jnp.broadcast_to(peak, (seqs, LANES)), (1, 0))[:1, :],
-        axis=1,
-        keepdims=True,
-    )
+    experts = scale_ref.shape[1]
+    peaks = jnp.transpose(jnp.broadcast_to(peak, (seqs, LANES)), (1, 0))[:1]
+    scales = jnp.sum(pick_ref[...] * peaks, axis=1, keepdims=True)
+    scales = jnp.transpose(jnp.broadcast_to(scales, (CAP * experts, LANES)), (1, 0))[:1]
+    for c in range(CAP):
+        scale_ref[c : c + 1, :] = scales[:, c * experts : (c + 1) * experts]
+    picks = [pick_ref[c * experts : (c + 1) * experts, :] for c in range(CAP)]
+    pick = jnp.concatenate([p[:, None, :] for p in picks], axis=1)
+    pick = pick.reshape(CAP * experts, seqs).astype(jnp.bfloat16)
     for c in range(half):
         own, other = own_ref[c, :, :part], other_ref[c, :, :part]
         pair = jnp.concatenate(
             [jnp.where(north, other, own), jnp.where(north, own, other)], axis=1
         )
         coded = (pair.astype(jnp.float32) * factor).astype(jnp.bfloat16)
-        out_ref[:, c * cols : (c + 1) * cols] = jnp.dot(
-            pick, coded, preferred_element_type=jnp.float32
-        ).astype(jnp.bfloat16)
+        rows = jnp.dot(pick, coded, preferred_element_type=jnp.float32).astype(jnp.bfloat16)
+        out_ref[:, :, c * cols : (c + 1) * cols] = rows.reshape(experts, CAP, cols)
 
 
 def whole_heads(
@@ -377,13 +446,20 @@
     def across_chips(value):
         return lax.all_to_all(value, "kv", 0, 0, axis_index_groups=chips, tiled=True)
 
-    gathered = queries.reshape(1, seq_count, width)
-    for bit in reversed(range(1, kv_count.bit_length() - 1)):
-        gathered = jnp.concatenate([gathered, from_partner(gathered, "kv", bit)], axis=0)
-    other_core = from_partner(gathered, "kv", 0)
+    orders = exchange_orders(kv_count.bit_length() - 1)
+    pieces = [queries.reshape(1, seq_count, width)]
+    others = [from_partner(pieces[0], "kv", 0)]
+    for steps in zip(*orders):
+        sent = pieces[0] if len(pieces) == 1 else joined(pieces)
+        pieces.append(from_crossing(sent, steps))
+        others.append(from_partner(pieces[-1], "kv", 0))
+    pieces = pieces + others
 
     payload = H * LAT // kv_count + LANES
     block = (half, seq_count, payload)
+    entry = LAT + ROPE
+    tiles = (entry + LANES - 1) // LANES
+    rows = kv_count * seq_count
     keep, send = pl.pallas_call(
         attend,
         name="attend",
@@ -391,14 +467,14 @@
             jax.ShapeDtypeStruct(block, jnp.float32),
             jax.ShapeDtypeStruct(block, jnp.bfloat16),
         ),
-        in_specs=[smem, smem] + whole(3),
+        in_specs=[smem, smem] + whole(1 + len(pieces)),
         out_specs=tuple(whole(2)),
         scratch_shapes=[
-            pltpu.VMEM((width // LANES, kv_count * seq_count, LANES), jnp.float32),
-            pltpu.VMEM((payload // LANES, kv_count * seq_count, LANES), jnp.float32),
+            pltpu.VMEM((H // kv_count, tiles, rows, LANES), jnp.float32),
+            pltpu.VMEM((payload // LANES, rows, LANES), jnp.float32),
         ],
-        compiler_params=params(),
-    )(place, context_lengths, gathered, other_core, latent_cache)
+        compiler_params=params(14),
+    )(place, context_lengths, jnp.swapaxes(latent_cache, 1, 2), *pieces)
     got = from_partner(send, "kv", 0)
     merged = pl.pallas_call(
         merge_pair,
@@ -438,27 +514,29 @@
     other = from_partner(own, "kv", 0)
 
     experts_local = EXPERTS // kv_count
-    slot_count = experts_local * CAP
-    targets = slot_targets(expert_ids)
-    own_match = slot_match(targets, shard_index * slot_count, slot_count)
-    own_pick = token_picker(own_match, seq_count)
-    slot_gate = jnp.sum(own_match * gate_weights.reshape(1, -1), axis=1)
+    pick, slot_gate = pl.pallas_call(
+        route,
+        name="route",
+        out_shape=(
+            jax.ShapeDtypeStruct((CAP * experts_local, seq_count), jnp.float32),
+            jax.ShapeDtypeStruct((CAP, experts_local), jnp.float32),
+        ),
+        in_specs=[smem] + whole(2),
+        out_specs=tuple(whole(2)),
+        compiler_params=params(),
+    )(place, expert_ids.T, gate_weights.T)
     dispatched, slot_scale = pl.pallas_call(
         finish,
         name="finish",
         out_shape=(
-            jax.ShapeDtypeStruct((slot_count, out_proj.shape[1]), jnp.bfloat16),
-            jax.ShapeDtypeStruct((slot_count, 1), jnp.float32),
+            jax.ShapeDtypeStruct((experts_local, CAP, out_proj.shape[1]), jnp.bfloat16),
+            jax.ShapeDtypeStruct((CAP, experts_local), jnp.float32),
         ),
         in_specs=[smem] + whole(3),
         out_specs=tuple(whole(2)),
         compiler_params=params(),
-    )(place, own, other, own_pick.astype(jnp.bfloat16))
-    return (
-        dispatched.reshape(experts_local, CAP, out_proj.shape[1]),
-        slot_scale.reshape(experts_local, CAP),
-        slot_gate.reshape(experts_local, CAP),
-    )
+    )(place, own, other, pick)
+    return dispatched, slot_scale.T, slot_gate.T
 
 
 def per_device(*args):

time: 137 us -> 102 us (0.74)
  Pallas kernels: 30.1 us -> 13.6 us
  blocking collectives: 27.1 us -> 40.4 us
  local copies, waits for them, and re-layouts: 16.6 us -> 3.36 us
  waiting for transfers between devices: 40.5 us -> 28.8 us
  other arithmetic: 6.7 us -> 0.83 us
    ppermute x7, waiting for transfers between devices: 21.8 us -> 5.67 us  [from_partner(): return lax.ppermute(value, axis, pairs)]
    all_to_all x1 -> x2, blocking collectives: 27.1 us -> 40.4 us  [across_chips(): lax.all_to_all(value, 'kv', 0, 0, axis_index_groups=chips, tiled=True)]
    ppermute x0 -> x3, waiting for transfers between devices: none -> 12.5 us  [from_crossing(): return lax.ppermute(value, 'kv', pairs)]
    pallas_call x1, Pallas kernels: 17.2 us -> 6.59 us  [whole_heads(): pl.pallas_call(attend, name='attend', out_shape=(jax.ShapeDtypeStruct(blo...]
    unnamed x23 -> x16, local copies, waits for them, and re-layouts: 13.5 us -> 3.36 us
    ppermute x0 -> x3, starting transfers between devices: none -> 8.87 us  [from_crossing(): return lax.ppermute(value, 'kv', pairs)]
    all_to_all x2 -> x1, waiting for transfers between devices: 18.7 us -> 10.6 us  [across_chips(): lax.all_to_all(value, 'kv', 0, 0, axis_index_groups=chips, tiled=True)]
    ppermute x7, starting transfers between devices: 7 us -> 1.3 us  [from_partner(): return lax.ppermute(value, axis, pairs)]
  transfers between devices with their start and end apart: 9 -> 11, of which waited for: 8 -> 9; matrix products, arithmetic and copies ran while one was open for 9% -> 0% of each run, Pallas kernels for 0% -> 1%
where the time goes in v2:
time: 102 us; the launch traced here: 101 us
  blocking collectives  40.4 us (40%)
  waiting for transfers between devices  28.8 us (28%)
  starting transfers between devices  13.8 us (14%)
  Pallas kernels  13.6 us (13%)
  local copies, waits for them, and re-layouts  3.36 us (3%)
    all_to_all x2, blocking collectives, across_chips(): lax.all_to_all(value, 'kv', 0, 0, axis_index_groups=chips, tiled=True)  40.4 us
    ppermute x3, waiting for transfers between devices, from_crossing(): return lax.ppermute(value, 'kv', pairs)  12.5 us
    all_to_all x1, waiting for transfers between devices, across_chips(): lax.all_to_all(value, 'kv', 0, 0, axis_index_groups=chips, tiled=True)  10.6 us
    ppermute x3, starting transfers between devices, from_crossing(): return lax.ppermute(value, 'kv', pairs)  8.87 us
    pallas_call x1, Pallas kernels, whole_heads(): pl.pallas_call(attend, name='attend', out_shape=(jax.ShapeDtypeStruct(blo...  6.59 us
    ppermute x7, waiting for transfers between devices, from_partner(): return lax.ppermute(value, axis, pairs)  5.67 us
    all_to_all x1, starting transfers between devices, across_chips(): lax.all_to_all(value, 'kv', 0, 0, axis_index_groups=chips, tiled=True)  3.59 us
    unnamed x16, local copies, waits for them, and re-layouts  3.36 us
  transfers between devices with their start and end apart: 11, of which 9 were waited for; matrix products, arithmetic and copies ran while one was open for 0% of the time, Pallas kernels for 1%

profile of v2, /device:TPU:0, one launch (start us, length us, event | category | flops | bytes accessed | tf_op | source)
XLA Modules:
  0.0 101.5 jit_solution(3066685604940719820)
XLA Ops:
  0.6 3.1 %collective-permute-start = (bf16[1,40,1152]{2,1,0:T(8,128)(2,1)}, bf16[1,40,1152]{2,1,0:T(8,128)(2,1)S(1)}, u32[]{:S(2)}, u32[]{:S(2)}) collective-permute-start(bf16[1,40,1152]{2,1,0:T(8,128)(2,1)} %bitcast.2.refs_0_), channel_id=1, source_target_pairs={{0,2},{1,9},{2,0},{3,11},{4,6},{5,13},{6,4},{7,15},{8,10},{9,1},{1... | collective-permute-start | bytes 276488 | tf_op jit(solution)/shard_map/ppermute | solution.py:150
  3.7 2.7 %collective-permute-done.refs_1_ = bf16[1,40,1152]{2,1,0:T(8,128)(2,1)S(1)} collective-permute-done((bf16[1,40,1152]{2,1,0:T(8,128)(2,1)}, bf16[1,40,1152]{2,1,0:T(8,128)(2,1)S(1)}, u32[]{:S(2)}, u32[]{:S(2)}) %collective-permute-start) | collective-permute-done | bytes 92192 | tf_op jit(solution)/shard_map/ppermute | solution.py:150
  6.4 0.9 join.2
  7.3 3.2 %collective-permute-start.1 = (bf16[2,40,1152]{2,1,0:T(8,128)(2,1)S(1)}, bf16[2,40,1152]{2,1,0:T(8,128)(2,1)S(1)}, u32[]{:S(2)}, u32[]{:S(2)}) collective-permute-start(bf16[2,40,1152]{2,1,0:T(8,128)(2,1)S(1)} %join.2), channel_id=1, source_target_pairs={{0,8},{1,5},{2,10},{3,7},{4,12},{5,1},{6,14},{7,3},{8,0},{9,13},{1... | collective-permute-start | bytes 552968 | tf_op jit(solution)/shard_map/ppermute | solution.py:150
  10.5 4.2 %collective-permute-done.1.refs_2_ = bf16[2,40,1152]{2,1,0:T(8,128)(2,1)S(1)} collective-permute-done((bf16[2,40,1152]{2,1,0:T(8,128)(2,1)S(1)}, bf16[2,40,1152]{2,1,0:T(8,128)(2,1)S(1)}, u32[]{:S(2)}, u32[]{:S(2)}) %collective-permute-start.1) | collective-permute-done | bytes 184352 | tf_op jit(solution)/shard_map/ppermute | solution.py:150
  14.7 0.9 join.3
  15.7 2.7 %collective-permute-start.2 = (bf16[4,40,1152]{2,1,0:T(8,128)(2,1)S(1)}, bf16[4,40,1152]{2,1,0:T(8,128)(2,1)S(1)}, u32[]{:S(2)}, u32[]{:S(2)}) collective-permute-start(bf16[4,40,1152]{2,1,0:T(8,128)(2,1)S(1)} %join.3), channel_id=1, source_target_pairs={{0,4},{1,3},{2,6},{3,1},{4,0},{5,7},{6,2},{7,5},{8,12},{9,11},{10,... | collective-permute-start | bytes 1105928 | tf_op jit(solution)/shard_map/ppermute | solution.py:150
  18.3 5.5 %collective-permute-done.2.refs_3_ = bf16[4,40,1152]{2,1,0:T(8,128)(2,1)S(1)} collective-permute-done((bf16[4,40,1152]{2,1,0:T(8,128)(2,1)S(1)}, bf16[4,40,1152]{2,1,0:T(8,128)(2,1)S(1)}, u32[]{:S(2)}, u32[]{:S(2)}) %collective-permute-start.2) | collective-permute-done | bytes 368672 | tf_op jit(solution)/shard_map/ppermute | solution.py:150
  23.8 0.0 collective-permute-start.6
  23.8 0.5 collective-permute-start.5
  24.3 0.0 collective-permute-start.3
  24.3 0.5 collective-permute-start.4
  24.8 1.1 %collective-permute-done.3.refs_4_ = bf16[1,40,1152]{2,1,0:T(8,128)(2,1)S(1)} collective-permute-done((bf16[1,40,1152]{2,1,0:T(8,128)(2,1)}, bf16[1,40,1152]{2,1,0:T(8,128)(2,1)S(1)}, u32[]{:S(2)}, u32[]{:S(2)}) %collective-permute-start.3) | collective-permute-done | bytes 92192 | tf_op jit(solution)/shard_map/ppermute | solution.py:26
  25.9 0.1 collective-permute-done.4.refs_5_
  26.0 0.0 collective-permute-done.5.refs_6_
  26.0 0.0 collective-permute-done.6.refs_7_
  26.0 0.0 copy-start
  26.0 2.7 %copy-done = bf16[40,128,576]{1,2,0:T(8,128)(2,1)S(1)} copy-done((bf16[40,128,576]{1,2,0:T(8,128)(2,1)S(1)}, bf16[40,128,576]{1,2,0:T(8,128)(2,1)}, u32[]{:S(2)}) %copy-start) | copy-done | bytes 5898264
  28.7 0.0 copy-start.6
  28.7 0.7 copy-done.6
  29.4 6.6 %attend.1 = (f32[8,40,1152]{2,1,0:T(8,128)S(1)}, bf16[8,40,1152]{2,1,0:T(8,128)(2,1)S(1)}) custom-call(s32[1]{0:T(128)} %bitcast.place_ref, s32[40]{0:T(128)S(1)} %copy-done.6, bf16[40,576,128]{2,1,0:T(8,128)(2,1)S(1)} %bitcast.7, bf16[1,40,1152]{2,1,0:T(8,128)(2,1)} %bitcast.2.refs_0_, bf16[1,40,1152]{2,1,0:T(8,128)(2,1)S(1)} %collective-permute-done.refs_1_, ...), custom_call_target="tpu_custom_call" | custom-call | tf_op jit(solution)/shard_map/attend/pallas_call | solution.py:463
  36.0 0.0 copy-start.1
  36.0 0.0 copy-start.2
  36.0 0.2 collective-permute-start.7
  36.2 2.1 %collective-permute-done.7.got_ref = bf16[8,40,1152]{2,1,0:T(8,128)(2,1)S(1)} collective-permute-done((bf16[8,40,1152]{2,1,0:T(8,128)(2,1)S(1)}, bf16[8,40,1152]{2,1,0:T(8,128)(2,1)S(1)}, u32[]{:S(2)}, u32[]{:S(2)}) %collective-permute-start.7) | collective-permute-done | bytes 737312 | tf_op jit(solution)/shard_map/ppermute | solution.py:26
  38.3 1.5 %merge_pair.1 = bf16[8,40,1152]{2,1,0:T(8,128)(2,1)S(1)} custom-call(f32[8,40,1152]{2,1,0:T(8,128)S(1)} %get-tuple-element.11.keep_ref, bf16[8,40,1152]{2,1,0:T(8,128)(2,1)S(1)} %collective-permute-done.7.got_ref), custom_call_target="tpu_custom_call" | custom-call | tf_op jit(solution)/shard_map/merge_pair/pallas_call | solution.py:479
  39.8 26.0 %all_to_all.15.got_ref = bf16[8,40,1152]{2,1,0:T(8,128)(2,1)S(1)} all-to-all(bf16[8,40,1152]{2,1,0:T(8,128)(2,1)S(1)} %merge_pair.1), channel_id=1, replica_groups={{0,2,4,6,8,10,12,14},{1,3,5,7,9,11,13,15},{16,18,20,22,24,26,28,30},{17..., dimensions={0} | all-to-all | bytes 1474560 | tf_op jit(solution)/shard_map/all_to_all | solution.py:447
  65.7 0.0 copy-done.1
  65.7 0.0 copy-done.2
  65.7 0.0 copy-start.7
  65.8 0.0 copy-start.4
  65.8 0.0 copy-start.5
  65.8 1.2 %project.1 = (f32[8,40,512]{2,1,0:T(8,128)S(1)}, bf16[8,40,512]{2,1,0:T(8,128)(2,1)S(1)}) custom-call(s32[1]{0:T(128)} %bitcast.place_ref, bf16[8,40,1152]{2,1,0:T(8,128)(2,1)S(1)} %all_to_all.15.got_ref, bf16[1024,128]{1,0:T(8,128)(2,1)S(1)} %copy-done.2, bf16[256,7168]{1,0:T(8,128)(2,1)S(1)} %copy-done.1), custom_call_target="tpu_custom_call" | custom-call | tf_op jit(solution)/shard_map/project/pallas_call | solution.py:492
  67.0 0.1 collective-permute-start.8
  67.1 1.6 %collective-permute-done.8 = bf16[8,40,512]{2,1,0:T(8,128)(2,1)S(1)} collective-permute-done((bf16[8,40,512]{2,1,0:T(8,128)(2,1)S(1)}, bf16[8,40,512]{2,1,0:T(8,128)(2,1)S(1)}, u32[]{:S(2)}, u32[]{:S(2)}) %collective-permute-start.8) | collective-permute-done | bytes 327712 | tf_op jit(solution)/shard_map/ppermute | solution.py:26
  68.7 0.8 add_convert_fusion
  69.5 3.6 %all-to-all-start.1 = ((bf16[8,40,512]{2,1,0:T(8,128)(2,1)}), bf16[8,40,512]{2,1,0:T(8,128)(2,1)S(1)}, u32[]{:S(2)}, u32[]{:S(2)}) async-start(bf16[8,40,512]{2,1,0:T(8,128)(2,1)} %add_convert_fusion), calls=%async_computation.1 | async-start | bytes 655360 | tf_op jit(solution)/shard_map/all_to_all | solution.py:447
  73.1 0.0 copy-done.7
  73.1 10.6 %all-to-all-done.1.got_ref = bf16[8,40,512]{2,1,0:T(8,128)(2,1)S(1)} async-done(((bf16[8,40,512]{2,1,0:T(8,128)(2,1)}), bf16[8,40,512]{2,1,0:T(8,128)(2,1)S(1)}, u32[]{:S(2)}, u32[]{:S(2)}) %all-to-all-start.1) | async-done | bytes 327712 | tf_op jit(solution)/shard_map/all_to_all | solution.py:447
  83.7 0.0 copy-done.3
  83.7 0.2 normalise.1
  84.0 14.4 %all_to_all.16.own_ref = bf16[8,40,512]{2,1,0:T(8,128)(2,1)S(1)} all-to-all(bf16[8,40,512]{2,1,0:T(8,128)(2,1)S(1)} %normalise.1), channel_id=1, replica_groups={{0,2,4,6,8,10,12,14},{1,3,5,7,9,11,13,15},{16,18,20,22,24,26,28,30},{17..., dimensions={0} | all-to-all | bytes 655360 | tf_op jit(solution)/shard_map/all_to_all | solution.py:447
  98.4 0.0 collective-permute-start.9
  98.4 0.0 copy-done.4
  98.4 0.0 copy-done.5
  98.4 0.8 route.1
  99.2 0.8 collective-permute-done.9.other_ref
  100.0 1.5 %finish.1 = (bf16[16,2,7168]{2,1,0:T(2,128)(2,1)}, f32[2,16]{1,0:T(2,128)}) custom-call(s32[1]{0:T(128)} %bitcast.place_ref, bf16[8,40,512]{2,1,0:T(8,128)(2,1)S(1)} %all_to_all.16.own_ref, bf16[8,40,512]{2,1,0:T(8,128)(2,1)S(1)} %collective-permute-done.9.other_ref, f32[32,40]{1,0:T(8,128)S(1)} %get-tuple-element.15.pick_ref), custom_call_target="tpu_custom_call" | custom-call | tf_op jit(solution)/shard_map/finish/pallas_call | solution.py:528
  (2 shorter events, 0.0 us)
Async XLA Ops:
  0.6 5.8 %collective-permute-start = (bf16[1,40,1152]{2,1,0:T(8,128)(2,1)}, bf16[1,40,1152]{2,1,0:T(8,128)(2,1)S(1)}, u32[]{:S(2)}, u32[]{:S(2)}) collective-permute-start(bf16[1,40,1152]{2,1,0:T(8,128)(2,1)} %bitcast.2.refs_0_), channel_id=1, source_target_pairs={{0,2},{1,9},{2,0},{3,11},{4,6},{5,13},{6,4},{7,15},{8,10},{9,1},{1... | collective-permute-start | bytes 276488 | tf_op jit(solution)/shard_map/ppermute | solution.py:150
  7.3 7.4 %collective-permute-start.1 = (bf16[2,40,1152]{2,1,0:T(8,128)(2,1)S(1)}, bf16[2,40,1152]{2,1,0:T(8,128)(2,1)S(1)}, u32[]{:S(2)}, u32[]{:S(2)}) collective-permute-start(bf16[2,40,1152]{2,1,0:T(8,128)(2,1)S(1)} %join.2), channel_id=1, source_target_pairs={{0,8},{1,5},{2,10},{3,7},{4,12},{5,1},{6,14},{7,3},{8,0},{9,13},{1... | collective-permute-start | bytes 552968 | tf_op jit(solution)/shard_map/ppermute | solution.py:150
  15.7 8.2 %collective-permute-start.2 = (bf16[4,40,1152]{2,1,0:T(8,128)(2,1)S(1)}, bf16[4,40,1152]{2,1,0:T(8,128)(2,1)S(1)}, u32[]{:S(2)}, u32[]{:S(2)}) collective-permute-start(bf16[4,40,1152]{2,1,0:T(8,128)(2,1)S(1)} %join.3), channel_id=1, source_target_pairs={{0,4},{1,3},{2,6},{3,1},{4,0},{5,7},{6,2},{7,5},{8,12},{9,11},{10,... | collective-permute-start | bytes 1105928 | tf_op jit(solution)/shard_map/ppermute | solution.py:150
  23.8 2.2 %collective-permute-start.6 = (bf16[4,40,1152]{2,1,0:T(8,128)(2,1)S(1)}, bf16[4,40,1152]{2,1,0:T(8,128)(2,1)S(1)}, u32[]{:S(2)}, u32[]{:S(2)}) collective-permute-start(bf16[4,40,1152]{2,1,0:T(8,128)(2,1)S(1)} %collective-permute-done.2.refs_3_), channel_id=1, source_target_pairs={{0,1},{1,0},{2,3},{3,2},{4,5},{5,4},{6,7},{7,6},{8,9},{9,8},{10,11... | collective-permute-start | bytes 1105928 | tf_op jit(solution)/shard_map/ppermute | solution.py:26
  23.8 2.2 %collective-permute-start.5 = (bf16[2,40,1152]{2,1,0:T(8,128)(2,1)S(1)}, bf16[2,40,1152]{2,1,0:T(8,128)(2,1)S(1)}, u32[]{:S(2)}, u32[]{:S(2)}) collective-permute-start(bf16[2,40,1152]{2,1,0:T(8,128)(2,1)S(1)} %collective-permute-done.1.refs_2_), channel_id=1, source_target_pairs={{0,1},{1,0},{2,3},{3,2},{4,5},{5,4},{6,7},{7,6},{8,9},{9,8},{10,11... | collective-permute-start | bytes 552968 | tf_op jit(solution)/shard_map/ppermute | solution.py:26
  24.3 1.6 %collective-permute-start.3 = (bf16[1,40,1152]{2,1,0:T(8,128)(2,1)}, bf16[1,40,1152]{2,1,0:T(8,128)(2,1)S(1)}, u32[]{:S(2)}, u32[]{:S(2)}) collective-permute-start(bf16[1,40,1152]{2,1,0:T(8,128)(2,1)} %bitcast.2.refs_0_), channel_id=1, source_target_pairs={{0,1},{1,0},{2,3},{3,2},{4,5},{5,4},{6,7},{7,6},{8,9},{9,8},{10,11... | collective-permute-start | bytes 276488 | tf_op jit(solution)/shard_map/ppermute | solution.py:26
  24.3 1.7 %collective-permute-start.4 = (bf16[1,40,1152]{2,1,0:T(8,128)(2,1)S(1)}, bf16[1,40,1152]{2,1,0:T(8,128)(2,1)S(1)}, u32[]{:S(2)}, u32[]{:S(2)}) collective-permute-start(bf16[1,40,1152]{2,1,0:T(8,128)(2,1)S(1)} %collective-permute-done.refs_1_), channel_id=1, source_target_pairs={{0,1},{1,0},{2,3},{3,2},{4,5},{5,4},{6,7},{7,6},{8,9},{9,8},{10,11... | collective-permute-start | bytes 276488 | tf_op jit(solution)/shard_map/ppermute | solution.py:26
  26.0 2.7 %copy-start = (bf16[40,128,576]{1,2,0:T(8,128)(2,1)S(1)}, bf16[40,128,576]{1,2,0:T(8,128)(2,1)}, u32[]{:S(2)}) copy-start(bf16[40,128,576]{1,2,0:T(8,128)(2,1)} %param.10) | copy-start | bytes 17694724
  28.7 0.7 copy-start.6
  36.0 29.8 %copy-start.1 = (bf16[256,7168]{1,0:T(8,128)(2,1)S(1)}, bf16[256,7168]{1,0:T(8,128)(2,1)}, u32[]{:S(2)}) copy-start(bf16[256,7168]{1,0:T(8,128)(2,1)} %proj_ref.1) | copy-start | bytes 11010052
  36.0 29.8 %copy-start.2 = (bf16[1024,128]{1,0:T(8,128)(2,1)S(1)}, bf16[1024,128]{1,0:T(8,128)(2,1)}, u32[]{:S(2)}) copy-start(bf16[1024,128]{1,0:T(8,128)(2,1)} %up_ref.1) | copy-start | bytes 786436
  36.0 2.3 %collective-permute-start.7 = (bf16[8,40,1152]{2,1,0:T(8,128)(2,1)S(1)}, bf16[8,40,1152]{2,1,0:T(8,128)(2,1)S(1)}, u32[]{:S(2)}, u32[]{:S(2)}) collective-permute-start(bf16[8,40,1152]{2,1,0:T(8,128)(2,1)S(1)} %get-tuple-element.12), channel_id=1, source_target_pairs={{0,1},{1,0},{2,3},{3,2},{4,5},{5,4},{6,7},{7,6},{8,9},{9,8},{10,11... | collective-permute-start | bytes 2211848 | tf_op jit(solution)/shard_map/ppermute | solution.py:26
  65.7 7.4 %copy-start.7 = (bf16[448]{0:T(512)(128)(2,1)S(1)}, bf16[448]{0:T(512)(128)(2,1)}, u32[]{:S(2)}) copy-start(bf16[448]{0:T(512)(128)(2,1)} %param.15) | copy-start | bytes 2692
  65.8 18.0 %copy-start.3 = (bf16[40,448]{1,0:T(8,128)(2,1)S(1)}, bf16[40,448]{1,0:T(8,128)(2,1)}, u32[]{:S(2)}) copy-start(bf16[40,448]{1,0:T(8,128)(2,1)} %residual_ref.1) | copy-start | bytes 107524
  65.8 32.6 %copy-start.4 = (s32[40,8]{0,1:T(8,128)S(1)}, s32[40,8]{0,1:T(8,128)}, u32[]{:S(2)}) copy-start(s32[40,8]{0,1:T(8,128)} %param.16) | copy-start | bytes 3844
  65.8 32.6 %copy-start.5 = (f32[40,8]{0,1:T(8,128)S(1)}, f32[40,8]{0,1:T(8,128)}, u32[]{:S(2)}) copy-start(f32[40,8]{0,1:T(8,128)} %param.17) | copy-start | bytes 3844
  67.0 1.7 %collective-permute-start.8 = (bf16[8,40,512]{2,1,0:T(8,128)(2,1)S(1)}, bf16[8,40,512]{2,1,0:T(8,128)(2,1)S(1)}, u32[]{:S(2)}, u32[]{:S(2)}) collective-permute-start(bf16[8,40,512]{2,1,0:T(8,128)(2,1)S(1)} %get-tuple-element.14), channel_id=1, source_target_pairs={{0,1},{1,0},{2,3},{3,2},{4,5},{5,4},{6,7},{7,6},{8,9},{9,8},{10,11... | collective-permute-start | bytes 983048 | tf_op jit(solution)/shard_map/ppermute | solution.py:26
  69.5 14.2 %all-to-all-start.1 = ((bf16[8,40,512]{2,1,0:T(8,128)(2,1)}), bf16[8,40,512]{2,1,0:T(8,128)(2,1)S(1)}, u32[]{:S(2)}, u32[]{:S(2)}) async-start(bf16[8,40,512]{2,1,0:T(8,128)(2,1)} %add_convert_fusion), calls=%async_computation.1 | async-start | bytes 655360 | tf_op jit(solution)/shard_map/all_to_all | solution.py:447
  98.4 1.6 %collective-permute-start.9 = (bf16[8,40,512]{2,1,0:T(8,128)(2,1)S(1)}, bf16[8,40,512]{2,1,0:T(8,128)(2,1)S(1)}, u32[]{:S(2)}, u32[]{:S(2)}) collective-permute-start(bf16[8,40,512]{2,1,0:T(8,128)(2,1)S(1)} %all_to_all.16.own_ref), channel_id=1, source_target_pairs={{0,1},{1,0},{2,3},{3,2},{4,5},{5,4},{6,7},{7,6},{8,9},{9,8},{10,11... | collective-permute-start | bytes 983048 | tf_op jit(solution)/shard_map/ppermute | solution.py:26

commit v3 on v2

--- a/solution.py
+++ b/solution.py
@@ -140,9 +140,14 @@
     return [pl.BlockSpec(memory_space=pltpu.VMEM) for _ in range(count)]
 
 
-def exchange_orders(width):
+def gather_orders(width):
     falling = list(range(width - 1, 0, -1))
     return [falling[-1:] + falling[:-1], falling]
+
+
+def scatter_orders(width):
+    rising = list(range(1, width))
+    return [rising, rising[1:] + rising[:1]]
 
 
 def from_crossing(value, steps):
@@ -155,6 +160,12 @@
     for step, bit in enumerate(order):
         mask ^= (position >> step) % 2 * 2 ** (bit - 1)
     return mask
+
+
+def landing(position, gather, scatter):
+    mask = distance(position, gather)
+    places = range(2 ** len(scatter))
+    return next(place for place in places if distance(place, scatter[::-1]) == mask)
 
 
 def join(*refs):
@@ -196,11 +207,21 @@
     return tile + pltpu.roll(tile, LANES - 32, axis) + pltpu.roll(tile, LANES - 64, axis)
 
 
-SEQS_AT_ONCE = 4
-
-
-def attend(place_ref, lengths_ref, cache_ref, *refs):
-    pieces, (keep_ref, send_ref, q_ref, o_ref) = refs[:-4], refs[-4:]
+SEQS_AT_ONCE = 8
+
+
+def attend(place_ref, lengths_hbm, cache_hbm, *refs):
+    pieces, refs = refs[:-8], refs[-8:]
+    keep_ref, send_ref, q_ref, o_ref, lengths_ref, cache_ref, length_done, cache_done = refs
+    length_copy = pltpu.make_async_copy(lengths_hbm, lengths_ref, length_done)
+    length_copy.start()
+
+    def cache_copy(number):
+        some = pl.ds(number * SEQS_AT_ONCE, SEQS_AT_ONCE)
+        return pltpu.make_async_copy(cache_hbm.at[some], cache_ref.at[some], cache_done.at[number])
+
+    for number in range(cache_done.shape[0]):
+        cache_copy(number).start()
     half, seqs, payload = keep_ref.shape
     blocks = 2 * half
     heads = H // blocks
@@ -218,8 +239,10 @@
     first = place_ref[0] * ctx_local
     position = first + lax.broadcasted_iota(jnp.int32, (H, ctx_local), 1)
     lane = lax.broadcasted_iota(jnp.int32, (blocks, LANES), 1)
+    length_copy.wait()
 
     def batch(number, carry):
+        cache_copy(number).wait()
         all_seqs = [number * SEQS_AT_ONCE + i for i in range(SEQS_AT_ONCE)]
         scores, tops, totals, weights, outs = [], [], [], [], []
         for seq in all_seqs:
@@ -262,16 +285,20 @@
         return carry
 
     lax.fori_loop(0, seqs // SEQS_AT_ONCE, batch, 0)
-    chip, north = place_ref[0] // 2, place_ref[0] % 2 == 1
-    orders = exchange_orders(blocks.bit_length() - 1)
+    north = place_ref[0] % 2 == 1
+    width = blocks.bit_length() - 1
+    gathers, scatters = gather_orders(width), scatter_orders(width)
     last = heads * LAT // LANES
     for block in range(half):
-        even, odd = (distance(block, order) for order in orders)
-        to = chip ^ jnp.where(north, odd, even)
+        even = landing(block, gathers[0], scatters[0])
+        odd = landing(block, gathers[1], scatters[1])
+        to = jnp.where(north, odd, even)
         at = block * seqs
         for t in range(last + 1):
             keep_ref[to, :, t * LANES : (t + 1) * LANES] = o_ref[t, at : at + seqs, :]
-        to = chip ^ jnp.where(north, even, odd)
+        even = landing(block, gathers[1], scatters[1])
+        odd = landing(block, gathers[0], scatters[0])
+        to = jnp.where(north, odd, even)
         at = (half + block) * seqs
         for t in range(last):
             cols = slice(t * LANES, (t + 1) * LANES)
@@ -279,51 +306,57 @@
         send_ref[to, :, heads * LAT :] = spread_stats(o_ref[last, at : at + seqs, :])
 
 
-def merge_pair(keep_ref, got_ref, out_ref):
-    half, seqs, width = keep_ref.shape
-    heads = (width - LANES) // LAT
-    lane = lax.broadcasted_iota(jnp.int32, (seqs, LANES), 1)
-
-    def step(block, carry):
-        mine = keep_ref[block, :, heads * LAT :]
-        theirs = gather_stats(got_ref[block, :, heads * LAT :])
-        stats = jnp.zeros((seqs, LANES), jnp.float32)
-        for h in range(heads):
-            top_a, top_b = mine[:, 2 * h : 2 * h + 1], theirs[:, 2 * h : 2 * h + 1]
-            sum_a, sum_b = mine[:, 2 * h + 1 : 2 * h + 2], theirs[:, 2 * h + 1 : 2 * h + 2]
-            top = jnp.maximum(top_a, top_b)
-            scale_a, scale_b = jnp.exp(top_a - top), jnp.exp(top_b - top)
-            total = sum_a * scale_a + sum_b * scale_b
-            cols = slice(h * LAT, (h + 1) * LAT)
-            out_ref[block, :, cols] = (
-                keep_ref[block, :, cols] * scale_a
-                + got_ref[block, :, cols].astype(jnp.float32) * scale_b
-            ).astype(jnp.bfloat16)
-            stats = jnp.where(lane == 2 * h, top, stats)
-            stats = jnp.where(lane == 2 * h + 1, total, stats)
+def merge_block(keep_ref, got_ref, block, heads):
+    mine = keep_ref[block, :, heads * LAT :]
+    theirs = gather_stats(got_ref[block, :, heads * LAT :])
+    lane = lax.broadcasted_iota(jnp.int32, mine.shape, 1)
+    stats, parts = jnp.zeros(mine.shape, jnp.float32), []
+    for h in range(heads):
+        top_a, top_b = mine[:, 2 * h : 2 * h + 1], theirs[:, 2 * h : 2 * h + 1]
+        sum_a, sum_b = mine[:, 2 * h + 1 : 2 * h + 2], theirs[:, 2 * h + 1 : 2 * h + 2]
+        top = jnp.maximum(top_a, top_b)
+        scale_a, scale_b = jnp.exp(top_a - top), jnp.exp(top_b - top)
+        cols = slice(h * LAT, (h + 1) * LAT)
+        parts.append(
+            keep_ref[block, :, cols] * scale_a
+            + got_ref[block, :, cols].astype(jnp.float32) * scale_b
+        )
+        stats = jnp.where(lane == 2 * h, top, stats)
+        stats = jnp.where(lane == 2 * h + 1, sum_a * scale_a + sum_b * scale_b, stats)
+    return parts, stats
+
+
+def merge_kept(keep_ref, got_ref, out_ref):
+    heads = (out_ref.shape[2] - LANES) // LAT
+    for block in range(out_ref.shape[0]):
+        parts, stats = merge_block(keep_ref, got_ref, block, heads)
+        for h, part in enumerate(parts):
+            out_ref[block, :, h * LAT : (h + 1) * LAT] = part
+        out_ref[block, :, heads * LAT :] = stats
+
+
+def merge_sent(keep_ref, got_ref, out_ref):
+    heads = (out_ref.shape[2] - LANES) // LAT
+    for block in range(out_ref.shape[0]):
+        parts, stats = merge_block(keep_ref, got_ref, out_ref.shape[0] + block, heads)
+        for h, part in enumerate(parts):
+            out_ref[block, :, h * LAT : (h + 1) * LAT] = part.astype(jnp.bfloat16)
         out_ref[block, :, heads * LAT :] = spread_stats(stats)
-        return carry
-
-    lax.fori_loop(0, half, step, 0, unroll=2)
-
-
-def project(place_ref, got_ref, up_ref, proj_ref, keep_ref, send_ref):
-    half, seqs, width = got_ref.shape
-    heads = (width - LANES) // LAT
-    stats = [gather_stats(got_ref[c, :, heads * LAT :]) for c in range(half)]
+
+
+def add_pair(keep_ref, got_ref, out_ref):
+    for block in range(keep_ref.shape[0]):
+        total = keep_ref[block] + got_ref[block].astype(jnp.float32)
+        out_ref[block] = total.astype(jnp.bfloat16)
+
+
+def project(place_ref, mine_ref, got_ref, up_ref, proj_ref, keep_ref, send_ref):
+    half, seqs, _ = keep_ref.shape
+    heads = (mine_ref.shape[2] - LANES) // LAT
+    parts, stats = merge_block(mine_ref, got_ref, 0, heads)
     values = []
-    for h in range(heads):
-        tops = [s[:, 2 * h : 2 * h + 1] for s in stats]
-        top = tops[0]
-        for t in tops[1:]:
-            top = jnp.maximum(top, t)
-        scales = [jnp.exp(t - top) for t in tops]
-        total = sum(s[:, 2 * h + 1 : 2 * h + 2] * x for s, x in zip(stats, scales))
-        merged = sum(
-            got_ref[c, :, h * LAT : (h + 1) * LAT].astype(jnp.float32) * scales[c]
-            for c in range(half)
-        )
-        merged = merged / total
+    for h, part in enumerate(parts):
+        merged = part / stats[:, 2 * h + 1 : 2 * h + 2]
         high = merged.astype(jnp.bfloat16)
         low = (merged - high.astype(jnp.float32)).astype(jnp.bfloat16)
         up = up_ref[h * LAT : (h + 1) * LAT, :]
@@ -442,15 +475,17 @@
     place = shard_index.reshape(1).astype(jnp.int32)
     chips = [[2 * c + core for c in range(half)] for core in range(2)]
     smem = pl.BlockSpec(memory_space=pltpu.SMEM)
+    hbm = pl.BlockSpec(memory_space=pltpu.HBM)
 
     def across_chips(value):
         return lax.all_to_all(value, "kv", 0, 0, axis_index_groups=chips, tiled=True)
 
-    orders = exchange_orders(kv_count.bit_length() - 1)
-    pieces = [queries.reshape(1, seq_count, width)]
-    others = [from_partner(pieces[0], "kv", 0)]
-    for steps in zip(*orders):
-        sent = pieces[0] if len(pieces) == 1 else joined(pieces)
+    bits = kv_count.bit_length() - 1
+    first = queries.reshape(1, seq_count, width)
+    pieces = [joined([first])]
+    others = [from_partner(first, "kv", 0)]
+    for steps in zip(*gather_orders(bits)):
+        sent = first if len(pieces) == 1 else joined(pieces)
         pieces.append(from_crossing(sent, steps))
         others.append(from_partner(pieces[-1], "kv", 0))
     pieces = pieces + others
@@ -467,24 +502,39 @@
             jax.ShapeDtypeStruct(block, jnp.float32),
             jax.ShapeDtypeStruct(block, jnp.bfloat16),
         ),
-        in_specs=[smem, smem] + whole(1 + len(pieces)),
+        in_specs=[smem, hbm, hbm] + whole(len(pieces)),
         out_specs=tuple(whole(2)),
         scratch_shapes=[
             pltpu.VMEM((H // kv_count, tiles, rows, LANES), jnp.float32),
             pltpu.VMEM((payload // LANES, rows, LANES), jnp.float32),
+            pltpu.SMEM((seq_count,), jnp.int32),
+            pltpu.VMEM((seq_count, entry, latent_cache.shape[1]), latent_cache.dtype),
+            pltpu.SemaphoreType.DMA,
+            pltpu.SemaphoreType.DMA((seq_count // SEQS_AT_ONCE,)),
         ],
-        compiler_params=params(14),
-    )(place, context_lengths, jnp.swapaxes(latent_cache, 1, 2), *pieces)
+        compiler_params=params(20),
+    )(
+        place,
+        pltpu.with_memory_space_constraint(context_lengths, pltpu.HBM),
+        pltpu.with_memory_space_constraint(jnp.swapaxes(latent_cache, 1, 2), pltpu.HBM),
+        *pieces,
+    )
     got = from_partner(send, "kv", 0)
-    merged = pl.pallas_call(
-        merge_pair,
-        name="merge_pair",
-        out_shape=jax.ShapeDtypeStruct(block, jnp.bfloat16),
-        in_specs=whole(2),
-        out_specs=whole(1)[0],
-        compiler_params=params(),
-    )(keep, got)
-    got = across_chips(merged)
+    for steps in zip(*scatter_orders(bits)):
+        count = keep.shape[0] // 2
+
+        def merged(kernel, dtype):
+            return pl.pallas_call(
+                kernel,
+                name=kernel.__name__,
+                out_shape=jax.ShapeDtypeStruct((count,) + keep.shape[1:], dtype),
+                in_specs=whole(2),
+                out_specs=whole(1)[0],
+                compiler_params=params(),
+            )(keep, got)
+
+        send, keep = merged(merge_sent, jnp.bfloat16), merged(merge_kept, jnp.float32)
+        got = from_crossing(send, steps)
 
     part = out_proj.shape[1] // kv_count
     padded = (part + 6 + LANES - 1) // LANES * LANES
@@ -496,12 +546,20 @@
             jax.ShapeDtypeStruct(strip, jnp.float32),
             jax.ShapeDtypeStruct(strip, jnp.bfloat16),
         ),
-        in_specs=[smem] + whole(3),
+        in_specs=[smem] + whole(4),
         out_specs=tuple(whole(2)),
         compiler_params=params(),
-    )(place, got, value_up, out_proj)
+    )(place, keep, got, value_up, out_proj)
     got = from_partner(send, "kv", 0)
-    got = across_chips((keep + got.astype(jnp.float32)).astype(jnp.bfloat16))
+    added = pl.pallas_call(
+        add_pair,
+        name="add_pair",
+        out_shape=jax.ShapeDtypeStruct(strip, jnp.bfloat16),
+        in_specs=whole(2),
+        out_specs=whole(1)[0],
+        compiler_params=params(),
+    )(keep, got)
+    got = across_chips(added)
     copies = pl.pallas_call(
         normalise,
         name="normalise",

time: 102 us -> 92.9 us (0.911)
  blocking collectives: 40.4 us -> 14.4 us
  waiting for transfers between devices: 28.8 us -> 40.7 us
  starting transfers between devices: 13.8 us -> 23 us
  local copies, waits for them, and re-layouts: 3.36 us -> 0.96 us
    all_to_all x2 -> x1, blocking collectives: 40.4 us -> 14.4 us  [across_chips(): lax.all_to_all(value, 'kv', 0, 0, axis_index_groups=chips, tiled=True)]
    ppermute x3 -> x6, waiting for transfers between devices: 12.5 us -> 24.5 us  [from_crossing(): return lax.ppermute(value, 'kv', pairs)]
    ppermute x3 -> x6, starting transfers between devices: 8.87 us -> 15.1 us  [from_crossing(): return lax.ppermute(value, 'kv', pairs)]
    all_to_all x1, starting transfers between devices: 3.59 us -> 6.61 us  [across_chips(): lax.all_to_all(value, 'kv', 0, 0, axis_index_groups=chips, tiled=True)]
    unnamed x16 -> x14, local copies, waits for them, and re-layouts: 3.36 us -> 0.96 us
    pallas_call x1 -> x7, Pallas kernels: 1.49 us -> 3.76 us  [the longest x6 2.98 us: merged(): pl.pallas_call(kernel, name=kernel.__name__, out_shape=jax.ShapeDtypeStru...]
    pallas_call x2 -> x3, Pallas kernels: 1.82 us -> 0.05 us  [joined(): pl.pallas_call(join, name='join', out_shape=jax.ShapeDtypeStruct((count,)...]
    pallas_call x1, Pallas kernels: 6.59 us -> 5.29 us  [whole_heads(): pl.pallas_call(attend, name='attend', out_shape=(jax.ShapeDtypeStruct(blo...]
  transfers between devices with their start and end apart: 11 -> 14, of which waited for: 9 -> 12; matrix products, arithmetic and copies ran while one was open for 0% -> 0% of each run, Pallas kernels for 1% -> 2%
where the time goes in v3:
time: 92.9 us; the launch traced here: 92.6 us
  waiting for transfers between devices  40.7 us (44%)
  starting transfers between devices  23 us (25%)
  blocking collectives  14.4 us (16%)
  Pallas kernels  12.8 us (14%)
  local copies, waits for them, and re-layouts  0.96 us (1%)
    ppermute x6, waiting for transfers between devices, from_crossing(): return lax.ppermute(value, 'kv', pairs)  24.5 us
    ppermute x6, starting transfers between devices, from_crossing(): return lax.ppermute(value, 'kv', pairs)  15.1 us
    all_to_all x1, blocking collectives, across_chips(): lax.all_to_all(value, 'kv', 0, 0, axis_index_groups=chips, tiled=True)  14.4 us
    all_to_all x1, waiting for transfers between devices, across_chips(): lax.all_to_all(value, 'kv', 0, 0, axis_index_groups=chips, tiled=True)  10.6 us
    all_to_all x1, starting transfers between devices, across_chips(): lax.all_to_all(value, 'kv', 0, 0, axis_index_groups=chips, tiled=True)  6.61 us
    ppermute x7, waiting for transfers between devices, from_partner(): return lax.ppermute(value, axis, pairs)  5.68 us
    pallas_call x1, Pallas kernels, whole_heads(): pl.pallas_call(attend, name='attend', out_shape=(jax.ShapeDtypeStruct(blo...  5.29 us
    pallas_call x6, Pallas kernels, merged(): pl.pallas_call(kernel, name=kernel.__name__, out_shape=jax.ShapeDtypeStru...  2.98 us
  transfers between devices with their start and end apart: 14, of which 12 were waited for; matrix products, arithmetic and copies ran while one was open for 0% of the time, Pallas kernels for 2%

profile of v3, /device:TPU:0, one launch (start us, length us, event | category | flops | bytes accessed | tf_op | source)
XLA Modules:
  0.0 92.6 jit_solution(14084523096536063772)
XLA Ops:
  0.6 3.1 %collective-permute-start = (bf16[1,40,1152]{2,1,0:T(8,128)(2,1)}, bf16[1,40,1152]{2,1,0:T(8,128)(2,1)S(1)}, u32[]{:S(2)}, u32[]{:S(2)}) collective-permute-start(bf16[1,40,1152]{2,1,0:T(8,128)(2,1)} %bitcast.7), channel_id=1, source_target_pairs={{0,2},{1,9},{2,0},{3,11},{4,6},{5,13},{6,4},{7,15},{8,10},{9,1},{1... | collective-permute-start | bytes 276488 | tf_op jit(solution)/shard_map/ppermute | solution.py:155
  3.7 0.9 copy-done.2
  4.6 1.8 %collective-permute-done.refs_1_ = bf16[1,40,1152]{2,1,0:T(8,128)(2,1)S(1)} collective-permute-done((bf16[1,40,1152]{2,1,0:T(8,128)(2,1)}, bf16[1,40,1152]{2,1,0:T(8,128)(2,1)S(1)}, u32[]{:S(2)}, u32[]{:S(2)}) %collective-permute-start) | collective-permute-done | bytes 92192 | tf_op jit(solution)/shard_map/ppermute | solution.py:155
  6.5 3.2 %collective-permute-start.1 = (bf16[2,40,1152]{2,1,0:T(8,128)(2,1)S(1)}, bf16[2,40,1152]{2,1,0:T(8,128)(2,1)S(1)}, u32[]{:S(2)}, u32[]{:S(2)}) collective-permute-start(bf16[2,40,1152]{2,1,0:T(8,128)(2,1)S(1)} %join.4), channel_id=1, source_target_pairs={{0,8},{1,5},{2,10},{3,7},{4,12},{5,1},{6,14},{7,3},{8,0},{9,13},{1... | collective-permute-start | bytes 552968 | tf_op jit(solution)/shard_map/ppermute | solution.py:155
  9.6 4.2 %collective-permute-done.1.refs_2_ = bf16[2,40,1152]{2,1,0:T(8,128)(2,1)S(1)} collective-permute-done((bf16[2,40,1152]{2,1,0:T(8,128)(2,1)S(1)}, bf16[2,40,1152]{2,1,0:T(8,128)(2,1)S(1)}, u32[]{:S(2)}, u32[]{:S(2)}) %collective-permute-start.1) | collective-permute-done | bytes 184352 | tf_op jit(solution)/shard_map/ppermute | solution.py:155
  13.9 2.7 %collective-permute-start.2 = (bf16[4,40,1152]{2,1,0:T(8,128)(2,1)S(1)}, bf16[4,40,1152]{2,1,0:T(8,128)(2,1)S(1)}, u32[]{:S(2)}, u32[]{:S(2)}) collective-permute-start(bf16[4,40,1152]{2,1,0:T(8,128)(2,1)S(1)} %join.5), channel_id=1, source_target_pairs={{0,4},{1,3},{2,6},{3,1},{4,0},{5,7},{6,2},{7,5},{8,12},{9,11},{10,... | collective-permute-start | bytes 1105928 | tf_op jit(solution)/shard_map/ppermute | solution.py:155
  16.5 5.5 %collective-permute-done.2.refs_3_ = bf16[4,40,1152]{2,1,0:T(8,128)(2,1)S(1)} collective-permute-done((bf16[4,40,1152]{2,1,0:T(8,128)(2,1)S(1)}, bf16[4,40,1152]{2,1,0:T(8,128)(2,1)S(1)}, u32[]{:S(2)}, u32[]{:S(2)}) %collective-permute-start.2) | collective-permute-done | bytes 368672 | tf_op jit(solution)/shard_map/ppermute | solution.py:155
  22.0 0.0 collective-permute-start.6
  22.0 0.5 collective-permute-start.5
  22.5 0.0 collective-permute-start.3
  22.5 0.5 collective-permute-start.4
  23.1 1.1 %collective-permute-done.3.refs_4_ = bf16[1,40,1152]{2,1,0:T(8,128)(2,1)S(1)} collective-permute-done((bf16[1,40,1152]{2,1,0:T(8,128)(2,1)}, bf16[1,40,1152]{2,1,0:T(8,128)(2,1)S(1)}, u32[]{:S(2)}, u32[]{:S(2)}) %collective-permute-start.3) | collective-permute-done | bytes 92192 | tf_op jit(solution)/shard_map/ppermute | solution.py:26
  24.1 0.1 collective-permute-done.4.refs_5_
  24.2 0.0 collective-permute-done.5.refs_6_
  24.3 0.0 collective-permute-done.6.refs_7_
  24.3 5.3 %attend.1 = (f32[8,40,1152]{2,1,0:T(8,128)S(1)}, bf16[8,40,1152]{2,1,0:T(8,128)(2,1)S(1)}) custom-call(s32[1]{0:T(128)} %bitcast.place_ref, s32[40]{0:T(128)} %lengths_hbm.1, bf16[40,576,128]{2,1,0:T(8,128)(2,1)} %bitcast.12, bf16[1,40,1152]{2,1,0:T(8,128)(2,1)S(1)} %join.3.refs_0_, bf16[1,40,1152]{2,1,0:T(8,128)(2,1)S(1)} %collective-permute-done.refs_1_, ...), custom_call_target="tpu_custom_call" | custom-call | tf_op jit(solution)/shard_map/attend/pallas_call | solution.py:498
  29.6 0.2 collective-permute-start.7
  29.8 2.1 %collective-permute-done.7.got_ref = bf16[8,40,1152]{2,1,0:T(8,128)(2,1)S(1)} collective-permute-done((bf16[8,40,1152]{2,1,0:T(8,128)(2,1)S(1)}, bf16[8,40,1152]{2,1,0:T(8,128)(2,1)S(1)}, u32[]{:S(2)}, u32[]{:S(2)}) %collective-permute-start.7) | collective-permute-done | bytes 737312 | tf_op jit(solution)/shard_map/ppermute | solution.py:26
  31.8 1.1 %merge_sent.3 = bf16[4,40,1152]{2,1,0:T(8,128)(2,1)S(1)} custom-call(f32[8,40,1152]{2,1,0:T(8,128)S(1)} %get-tuple-element.11.keep_ref, bf16[8,40,1152]{2,1,0:T(8,128)(2,1)S(1)} %collective-permute-done.7.got_ref), custom_call_target="tpu_custom_call" | custom-call | tf_op jit(solution)/shard_map/merge_sent/pallas_call | solution.py:527
  32.9 0.0 copy-start.1
  32.9 1.6 %collective-permute-start.8 = (bf16[4,40,1152]{2,1,0:T(8,128)(2,1)S(1)}, bf16[4,40,1152]{2,1,0:T(8,128)(2,1)S(1)}, u32[]{:S(2)}, u32[]{:S(2)}) collective-permute-start(bf16[4,40,1152]{2,1,0:T(8,128)(2,1)S(1)} %merge_sent.3), channel_id=1, source_target_pairs={{0,2},{1,5},{2,0},{3,7},{4,6},{5,1},{6,4},{7,3},{8,10},{9,13},{10,... | collective-permute-start | bytes 1105928 | tf_op jit(solution)/shard_map/ppermute | solution.py:155
  34.5 0.7 merge_kept.3.keep_ref
  35.2 5.3 %collective-permute-done.8.got_ref = bf16[4,40,1152]{2,1,0:T(8,128)(2,1)S(1)} collective-permute-done((bf16[4,40,1152]{2,1,0:T(8,128)(2,1)S(1)}, bf16[4,40,1152]{2,1,0:T(8,128)(2,1)S(1)}, u32[]{:S(2)}, u32[]{:S(2)}) %collective-permute-start.8) | collective-permute-done | bytes 368672 | tf_op jit(solution)/shard_map/ppermute | solution.py:155
  40.5 0.4 merge_sent.4
  40.9 2.1 %collective-permute-start.9 = (bf16[2,40,1152]{2,1,0:T(8,128)(2,1)S(1)}, bf16[2,40,1152]{2,1,0:T(8,128)(2,1)S(1)}, u32[]{:S(2)}, u32[]{:S(2)}) collective-permute-start(bf16[2,40,1152]{2,1,0:T(8,128)(2,1)S(1)} %merge_sent.4), channel_id=1, source_target_pairs={{0,4},{1,9},{2,6},{3,11},{4,0},{5,13},{6,2},{7,15},{8,12},{9,1},{1... | collective-permute-start | bytes 552968 | tf_op jit(solution)/shard_map/ppermute | solution.py:155
  43.0 0.3 merge_kept.4.keep_ref
  43.3 0.0 copy-start.6
  43.3 0.0 copy-start.3
  43.3 5.0 %collective-permute-done.9.got_ref = bf16[2,40,1152]{2,1,0:T(8,128)(2,1)S(1)} collective-permute-done((bf16[2,40,1152]{2,1,0:T(8,128)(2,1)S(1)}, bf16[2,40,1152]{2,1,0:T(8,128)(2,1)S(1)}, u32[]{:S(2)}, u32[]{:S(2)}) %collective-permute-start.9) | collective-permute-done | bytes 184352 | tf_op jit(solution)/shard_map/ppermute | solution.py:155
  48.3 0.3 merge_sent.5
  48.6 2.5 %collective-permute-start.10 = (bf16[1,40,1152]{2,1,0:T(8,128)(2,1)S(1)}, bf16[1,40,1152]{2,1,0:T(8,128)(2,1)S(1)}, u32[]{:S(2)}, u32[]{:S(2)}) collective-permute-start(bf16[1,40,1152]{2,1,0:T(8,128)(2,1)S(1)} %merge_sent.5), channel_id=1, source_target_pairs={{0,8},{1,3},{2,10},{3,1},{4,12},{5,7},{6,14},{7,5},{8,0},{9,11},{1... | collective-permute-start | bytes 276488 | tf_op jit(solution)/shard_map/ppermute | solution.py:155
  51.1 0.2 merge_kept.5.mine_ref
  51.3 0.0 copy-start.4
  51.3 0.0 copy-start.5
  51.4 2.7 %collective-permute-done.10.got_ref = bf16[1,40,1152]{2,1,0:T(8,128)(2,1)S(1)} collective-permute-done((bf16[1,40,1152]{2,1,0:T(8,128)(2,1)S(1)}, bf16[1,40,1152]{2,1,0:T(8,128)(2,1)S(1)}, u32[]{:S(2)}, u32[]{:S(2)}) %collective-permute-start.10) | collective-permute-done | bytes 92192 | tf_op jit(solution)/shard_map/ppermute | solution.py:155
  54.0 0.0 copy-done
  54.0 1.2 %project.1 = (f32[8,40,512]{2,1,0:T(8,128)S(1)}, bf16[8,40,512]{2,1,0:T(8,128)(2,1)S(1)}) custom-call(s32[1]{0:T(128)} %bitcast.place_ref, f32[1,40,1152]{2,1,0:T(8,128)S(1)} %merge_kept.5.mine_ref, bf16[1,40,1152]{2,1,0:T(8,128)(2,1)S(1)} %collective-permute-done.10.got_ref, bf16[1024,128]{1,0:T(8,128)(2,1)S(1)} %copy-done.1, bf16[256,7168]{1,0:T(8,128)(2,1)S(1)} %copy-done), custom_call_target="tpu_custom_call" | custom-call | tf_op jit(solution)/shard_map/project/pallas_call | solution.py:542
  55.2 0.1 collective-permute-start.11
  55.3 1.6 %collective-permute-done.11.got_ref = bf16[8,40,512]{2,1,0:T(8,128)(2,1)S(1)} collective-permute-done((bf16[8,40,512]{2,1,0:T(8,128)(2,1)S(1)}, bf16[8,40,512]{2,1,0:T(8,128)(2,1)S(1)}, u32[]{:S(2)}, u32[]{:S(2)}) %collective-permute-start.11) | collective-permute-done | bytes 327712 | tf_op jit(solution)/shard_map/ppermute | solution.py:26
  56.9 0.8 add_pair.1
  57.7 6.6 %all-to-all-start = ((bf16[8,40,512]{2,1,0:T(8,128)(2,1)}), bf16[8,40,512]{2,1,0:T(8,128)(2,1)S(1)}, u32[]{:S(2)}, u32[]{:S(2)}) async-start(bf16[8,40,512]{2,1,0:T(8,128)(2,1)} %add_pair.1), calls=%async_computation | async-start | bytes 655360 | tf_op jit(solution)/shard_map/all_to_all | solution.py:481
  64.3 10.6 %all-to-all-done.got_ref = bf16[8,40,512]{2,1,0:T(8,128)(2,1)S(1)} async-done(((bf16[8,40,512]{2,1,0:T(8,128)(2,1)}), bf16[8,40,512]{2,1,0:T(8,128)(2,1)S(1)}, u32[]{:S(2)}, u32[]{:S(2)}) %all-to-all-start) | async-done | bytes 327712 | tf_op jit(solution)/shard_map/all_to_all | solution.py:481
  74.9 0.2 normalise.1
  75.1 14.4 %all_to_all.10.own_ref = bf16[8,40,512]{2,1,0:T(8,128)(2,1)S(1)} all-to-all(bf16[8,40,512]{2,1,0:T(8,128)(2,1)S(1)} %normalise.1), channel_id=1, replica_groups={{0,2,4,6,8,10,12,14},{1,3,5,7,9,11,13,15},{16,18,20,22,24,26,28,30},{17..., dimensions={0} | all-to-all | bytes 655360 | tf_op jit(solution)/shard_map/all_to_all | solution.py:481
  89.5 0.0 collective-permute-start.12
  89.5 0.8 route.1
  90.4 0.8 collective-permute-done.12.other_ref
  91.1 1.5 %finish.1 = (bf16[16,2,7168]{2,1,0:T(2,128)(2,1)}, f32[2,16]{1,0:T(2,128)}) custom-call(s32[1]{0:T(128)} %bitcast.place_ref, bf16[8,40,512]{2,1,0:T(8,128)(2,1)S(1)} %all_to_all.10.own_ref, bf16[8,40,512]{2,1,0:T(8,128)(2,1)S(1)} %collective-permute-done.12.other_ref, f32[32,40]{1,0:T(8,128)S(1)} %get-tuple-element.15.pick_ref), custom_call_target="tpu_custom_call" | custom-call | tf_op jit(solution)/shard_map/finish/pallas_call | solution.py:586
  (11 shorter events, 0.1 us)
Async XLA Ops:
  0.6 5.8 %collective-permute-start = (bf16[1,40,1152]{2,1,0:T(8,128)(2,1)}, bf16[1,40,1152]{2,1,0:T(8,128)(2,1)S(1)}, u32[]{:S(2)}, u32[]{:S(2)}) collective-permute-start(bf16[1,40,1152]{2,1,0:T(8,128)(2,1)} %bitcast.7), channel_id=1, source_target_pairs={{0,2},{1,9},{2,0},{3,11},{4,6},{5,13},{6,4},{7,15},{8,10},{9,1},{1... | collective-permute-start | bytes 276488 | tf_op jit(solution)/shard_map/ppermute | solution.py:155
  3.7 0.9 copy-start.2
  6.5 7.4 %collective-permute-start.1 = (bf16[2,40,1152]{2,1,0:T(8,128)(2,1)S(1)}, bf16[2,40,1152]{2,1,0:T(8,128)(2,1)S(1)}, u32[]{:S(2)}, u32[]{:S(2)}) collective-permute-start(bf16[2,40,1152]{2,1,0:T(8,128)(2,1)S(1)} %join.4), channel_id=1, source_target_pairs={{0,8},{1,5},{2,10},{3,7},{4,12},{5,1},{6,14},{7,3},{8,0},{9,13},{1... | collective-permute-start | bytes 552968 | tf_op jit(solution)/shard_map/ppermute | solution.py:155
  13.9 8.2 %collective-permute-start.2 = (bf16[4,40,1152]{2,1,0:T(8,128)(2,1)S(1)}, bf16[4,40,1152]{2,1,0:T(8,128)(2,1)S(1)}, u32[]{:S(2)}, u32[]{:S(2)}) collective-permute-start(bf16[4,40,1152]{2,1,0:T(8,128)(2,1)S(1)} %join.5), channel_id=1, source_target_pairs={{0,4},{1,3},{2,6},{3,1},{4,0},{5,7},{6,2},{7,5},{8,12},{9,11},{10,... | collective-permute-start | bytes 1105928 | tf_op jit(solution)/shard_map/ppermute | solution.py:155
  22.0 2.2 %collective-permute-start.6 = (bf16[4,40,1152]{2,1,0:T(8,128)(2,1)S(1)}, bf16[4,40,1152]{2,1,0:T(8,128)(2,1)S(1)}, u32[]{:S(2)}, u32[]{:S(2)}) collective-permute-start(bf16[4,40,1152]{2,1,0:T(8,128)(2,1)S(1)} %collective-permute-done.2.refs_3_), channel_id=1, source_target_pairs={{0,1},{1,0},{2,3},{3,2},{4,5},{5,4},{6,7},{7,6},{8,9},{9,8},{10,11... | collective-permute-start | bytes 1105928 | tf_op jit(solution)/shard_map/ppermute | solution.py:26
  22.0 2.2 %collective-permute-start.5 = (bf16[2,40,1152]{2,1,0:T(8,128)(2,1)S(1)}, bf16[2,40,1152]{2,1,0:T(8,128)(2,1)S(1)}, u32[]{:S(2)}, u32[]{:S(2)}) collective-permute-start(bf16[2,40,1152]{2,1,0:T(8,128)(2,1)S(1)} %collective-permute-done.1.refs_2_), channel_id=1, source_target_pairs={{0,1},{1,0},{2,3},{3,2},{4,5},{5,4},{6,7},{7,6},{8,9},{9,8},{10,11... | collective-permute-start | bytes 552968 | tf_op jit(solution)/shard_map/ppermute | solution.py:26
  22.5 1.6 %collective-permute-start.3 = (bf16[1,40,1152]{2,1,0:T(8,128)(2,1)}, bf16[1,40,1152]{2,1,0:T(8,128)(2,1)S(1)}, u32[]{:S(2)}, u32[]{:S(2)}) collective-permute-start(bf16[1,40,1152]{2,1,0:T(8,128)(2,1)} %bitcast.8), channel_id=1, source_target_pairs={{0,1},{1,0},{2,3},{3,2},{4,5},{5,4},{6,7},{7,6},{8,9},{9,8},{10,11... | collective-permute-start | bytes 276488 | tf_op jit(solution)/shard_map/ppermute | solution.py:26
  22.5 1.7 %collective-permute-start.4 = (bf16[1,40,1152]{2,1,0:T(8,128)(2,1)S(1)}, bf16[1,40,1152]{2,1,0:T(8,128)(2,1)S(1)}, u32[]{:S(2)}, u32[]{:S(2)}) collective-permute-start(bf16[1,40,1152]{2,1,0:T(8,128)(2,1)S(1)} %collective-permute-done.refs_1_), channel_id=1, source_target_pairs={{0,1},{1,0},{2,3},{3,2},{4,5},{5,4},{6,7},{7,6},{8,9},{9,8},{10,11... | collective-permute-start | bytes 276488 | tf_op jit(solution)/shard_map/ppermute | solution.py:26
  29.6 2.3 %collective-permute-start.7 = (bf16[8,40,1152]{2,1,0:T(8,128)(2,1)S(1)}, bf16[8,40,1152]{2,1,0:T(8,128)(2,1)S(1)}, u32[]{:S(2)}, u32[]{:S(2)}) collective-permute-start(bf16[8,40,1152]{2,1,0:T(8,128)(2,1)S(1)} %get-tuple-element.12), channel_id=1, source_target_pairs={{0,1},{1,0},{2,3},{3,2},{4,5},{5,4},{6,7},{7,6},{8,9},{9,8},{10,11... | collective-permute-start | bytes 2211848 | tf_op jit(solution)/shard_map/ppermute | solution.py:26
  32.9 21.1 %copy-start = (bf16[256,7168]{1,0:T(8,128)(2,1)S(1)}, bf16[256,7168]{1,0:T(8,128)(2,1)}, u32[]{:S(2)}) copy-start(bf16[256,7168]{1,0:T(8,128)(2,1)} %proj_ref.1) | copy-start | bytes 11010052
  32.9 21.1 %copy-start.1 = (bf16[1024,128]{1,0:T(8,128)(2,1)S(1)}, bf16[1024,128]{1,0:T(8,128)(2,1)}, u32[]{:S(2)}) copy-start(bf16[1024,128]{1,0:T(8,128)(2,1)} %up_ref.1) | copy-start | bytes 786436
  32.9 7.6 %collective-permute-start.8 = (bf16[4,40,1152]{2,1,0:T(8,128)(2,1)S(1)}, bf16[4,40,1152]{2,1,0:T(8,128)(2,1)S(1)}, u32[]{:S(2)}, u32[]{:S(2)}) collective-permute-start(bf16[4,40,1152]{2,1,0:T(8,128)(2,1)S(1)} %merge_sent.3), channel_id=1, source_target_pairs={{0,2},{1,5},{2,0},{3,7},{4,6},{5,1},{6,4},{7,3},{8,10},{9,13},{10,... | collective-permute-start | bytes 1105928 | tf_op jit(solution)/shard_map/ppermute | solution.py:155
  40.9 7.4 %collective-permute-start.9 = (bf16[2,40,1152]{2,1,0:T(8,128)(2,1)S(1)}, bf16[2,40,1152]{2,1,0:T(8,128)(2,1)S(1)}, u32[]{:S(2)}, u32[]{:S(2)}) collective-permute-start(bf16[2,40,1152]{2,1,0:T(8,128)(2,1)S(1)} %merge_sent.4), channel_id=1, source_target_pairs={{0,4},{1,9},{2,6},{3,11},{4,0},{5,13},{6,2},{7,15},{8,12},{9,1},{1... | collective-permute-start | bytes 552968 | tf_op jit(solution)/shard_map/ppermute | solution.py:155
  43.3 21.1 %copy-start.6 = (bf16[448]{0:T(512)(128)(2,1)S(1)}, bf16[448]{0:T(512)(128)(2,1)}, u32[]{:S(2)}) copy-start(bf16[448]{0:T(512)(128)(2,1)} %param.15) | copy-start | bytes 2692
  43.3 31.6 %copy-start.3 = (bf16[40,448]{1,0:T(8,128)(2,1)S(1)}, bf16[40,448]{1,0:T(8,128)(2,1)}, u32[]{:S(2)}) copy-start(bf16[40,448]{1,0:T(8,128)(2,1)} %residual_ref.1) | copy-start | bytes 107524
  48.6 5.5 %collective-permute-start.10 = (bf16[1,40,1152]{2,1,0:T(8,128)(2,1)S(1)}, bf16[1,40,1152]{2,1,0:T(8,128)(2,1)S(1)}, u32[]{:S(2)}, u32[]{:S(2)}) collective-permute-start(bf16[1,40,1152]{2,1,0:T(8,128)(2,1)S(1)} %merge_sent.5), channel_id=1, source_target_pairs={{0,8},{1,3},{2,10},{3,1},{4,12},{5,7},{6,14},{7,5},{8,0},{9,11},{1... | collective-permute-start | bytes 276488 | tf_op jit(solution)/shard_map/ppermute | solution.py:155
  51.3 38.2 %copy-start.4 = (s32[40,8]{0,1:T(8,128)S(1)}, s32[40,8]{0,1:T(8,128)}, u32[]{:S(2)}) copy-start(s32[40,8]{0,1:T(8,128)} %param.16) | copy-start | bytes 3844
  51.3 38.2 %copy-start.5 = (f32[40,8]{0,1:T(8,128)S(1)}, f32[40,8]{0,1:T(8,128)}, u32[]{:S(2)}) copy-start(f32[40,8]{0,1:T(8,128)} %param.17) | copy-start | bytes 3844
  55.2 1.7 %collective-permute-start.11 = (bf16[8,40,512]{2,1,0:T(8,128)(2,1)S(1)}, bf16[8,40,512]{2,1,0:T(8,128)(2,1)S(1)}, u32[]{:S(2)}, u32[]{:S(2)}) collective-permute-start(bf16[8,40,512]{2,1,0:T(8,128)(2,1)S(1)} %get-tuple-element.14), channel_id=1, source_target_pairs={{0,1},{1,0},{2,3},{3,2},{4,5},{5,4},{6,7},{7,6},{8,9},{9,8},{10,11... | collective-permute-start | bytes 983048 | tf_op jit(solution)/shard_map/ppermute | solution.py:26
  57.7 17.2 %all-to-all-start = ((bf16[8,40,512]{2,1,0:T(8,128)(2,1)}), bf16[8,40,512]{2,1,0:T(8,128)(2,1)S(1)}, u32[]{:S(2)}, u32[]{:S(2)}) async-start(bf16[8,40,512]{2,1,0:T(8,128)(2,1)} %add_pair.1), calls=%async_computation | async-start | bytes 655360 | tf_op jit(solution)/shard_map/all_to_all | solution.py:481
  89.5 1.6 %collective-permute-start.12 = (bf16[8,40,512]{2,1,0:T(8,128)(2,1)S(1)}, bf16[8,40,512]{2,1,0:T(8,128)(2,1)S(1)}, u32[]{:S(2)}, u32[]{:S(2)}) collective-permute-start(bf16[8,40,512]{2,1,0:T(8,128)(2,1)S(1)} %all_to_all.10.own_ref), channel_id=1, source_target_pairs={{0,1},{1,0},{2,3},{3,2},{4,5},{5,4},{6,7},{7,6},{8,9},{9,8},{10,11... | collective-permute-start | bytes 983048 | tf_op jit(solution)/shard_map/ppermute | solution.py:26
